TPU v7x, 16 devices: a whole 2x2x2 slice. The times are simulated.
16 devices in a mesh: dp: 2 (over z), tp: 8 (over y, x, core).
Axes of the slice: x: 2, y: 2, z: 2, core: 2. Of those that a mesh axis runs over, the one named last changes fastest.
Arguments:
- x_tokens: bfloat16 [32, 512, 3072], P('dp', 'tp'), parts along dimension 0
- e_time: float32 [32, 3, 3072], P('dp'), parts along dimension 0
- m_block: float32 [3, 3072], replicated
- w_q: bfloat16 [3072, 3072], P(None, 'tp')
- b_q: float32 [3072], P('tp')
- w_k: bfloat16 [3072, 3072], P(None, 'tp')
- b_k: float32 [3072], P('tp')
- w_v: bfloat16 [3072, 3072], P(None, 'tp')
- b_v: float32 [3072], P('tp')
- w_o: bfloat16 [3072, 3072], P('tp')
- b_o: float32 [3072], replicated
- g_q: float32 [3072], P('tp')
- g_k: float32 [3072], P('tp')
- positions: int32 [1024, 3], P('dp'), parts along dimension 0
- d_out: bfloat16 [32, 512, 3072], P('dp', 'tp'), parts along dimension 0
Outputs:
- output 1: bfloat16 [32, 512, 3072], P('dp', 'tp'), parts along dimension 0
- output 2: bfloat16 [32, 512, 3072], P('dp', 'tp'), parts along dimension 0
- output 3: float32 [32, 3, 3072], P('dp'), parts along dimension 0
- output 4: float32 [6, 3072], P('dp'), parts along dimension 0
- output 5: bfloat16 [6144, 3072], P('dp', 'tp'), parts along dimension 0
- output 6: bfloat16 [6144, 3072], P('dp', 'tp'), parts along dimension 0
- output 7: bfloat16 [6144, 3072], P('dp', 'tp'), parts along dimension 0
- output 8: bfloat16 [6144, 3072], P(('dp', 'tp')), parts along dimension 0
- output 9: float32 [6144], P(('dp', 'tp')), parts along dimension 0
- output 10: float32 [6144], P(('dp', 'tp')), parts along dimension 0
There are 2 independent parts. A program takes and returns all parts, laid end to end along the dimension named above; an argument that names none is the same for every part.
All inputs are finite; a program needn't handle non-finite values.
Results may differ from a plain program's by a relative error of at most 0.0197529.
Values are sent between devices in bfloat16 or wider.
A program may use at most 1 GiB of HBM per device.

v0:
```python
import jax
import jax.numpy as jnp
from jax import lax
from jax.sharding import PartitionSpec as P

HEAD_DIM = 128
EPS_NORM = 1e-6
ROPE_BASE = 10000.0
ROW_CONTRACT = (((0,), (0,)), ((), ()))
COL_CONTRACT = (((1,), (1,)), ((), ()))


def rope_angles(positions):
    half_dim = HEAD_DIM // 2
    side_len = HEAD_DIM // 6
    first_len = half_dim - 2 * side_len
    pair_idx = jnp.arange(half_dim)
    section = (pair_idx >= first_len).astype(jnp.int32) + (pair_idx >= first_len + side_len).astype(jnp.int32)
    offset = jnp.where(section == 0, 0, jnp.where(section == 1, first_len, first_len + side_len))
    sec_width = jnp.where(section == 0, first_len, side_len)
    freq_vals = ROPE_BASE ** (-(pair_idx - offset).astype(jnp.float32) / sec_width.astype(jnp.float32))
    select = jnp.where(section[None, :] == jnp.arange(3)[:, None], freq_vals[None, :], 0.0)
    angles = jnp.sum(positions.astype(jnp.float32)[:, :, None] * select[None, :, :], axis=1)
    return jnp.cos(angles), jnp.sin(angles)


def rope_rotate(values, cos_part, sin_part):
    val_pairs = values.reshape(values.shape[:-1] + (values.shape[-1] // 2, 2))
    even_part = val_pairs[..., 0]
    odd_part = val_pairs[..., 1]
    rotated = jnp.stack([even_part * cos_part - odd_part * sin_part, even_part * sin_part + odd_part * cos_part], axis=-1)
    return rotated.reshape(values.shape)


def attend(q_rot, k_rot, v_heads):
    scores = jnp.einsum('bqhd,bkhd->bhqk', q_rot, k_rot, preferred_element_type=jnp.float32) * HEAD_DIM ** -0.5
    attn_probs = jax.nn.softmax(scores, axis=-1).astype(jnp.bfloat16)
    return jnp.einsum('bhqk,bkhd->bqhd', attn_probs, v_heads, preferred_element_type=jnp.float32).astype(jnp.bfloat16)


def solution(mesh):
    tp_size = mesh.shape['tp']

    def device_step(x_loc, e_loc, m_block, w_q, b_q, w_k, b_k, w_v, b_v, w_o, b_o, g_q, g_k, pos_part, dy_loc):
        batch_size, seq_loc, model_dim = x_loc.shape
        seq_len = seq_loc * tp_size
        rows_all = batch_size * seq_len
        heads_loc = w_q.shape[1] // HEAD_DIM
        head_shape = (batch_size, seq_len, heads_loc, HEAD_DIM)
        cos_tab, sin_tab = rope_angles(pos_part)
        cos_bcast = cos_tab[None, :, None, :]
        sin_bcast = sin_tab[None, :, None, :]

        mod_rows = m_block[None] + e_loc
        shift_row = mod_rows[:, 0][:, None]
        scale_one = 1.0 + mod_rows[:, 1][:, None]
        gate_row = mod_rows[:, 2][:, None]
        x_float = x_loc.astype(jnp.float32)
        centered = x_float - jnp.mean(x_float, axis=-1, keepdims=True)
        inv_std = lax.rsqrt(jnp.mean(centered * centered, axis=-1, keepdims=True) + EPS_NORM)
        x_norm = centered * inv_std
        y_loc = (x_norm * scale_one + shift_row).astype(jnp.bfloat16)
        y_full = lax.all_gather(y_loc, 'tp', axis=1, tiled=True).reshape(rows_all, model_dim)

        q_raw = jnp.dot(y_full, w_q, preferred_element_type=jnp.float32) + b_q
        k_raw = jnp.dot(y_full, w_k, preferred_element_type=jnp.float32) + b_k
        v_heads = (jnp.dot(y_full, w_v, preferred_element_type=jnp.float32) + b_v).astype(jnp.bfloat16).reshape(head_shape)
        sq_sums = lax.psum(jnp.stack([jnp.sum(q_raw * q_raw, axis=-1), jnp.sum(k_raw * k_raw, axis=-1)]), 'tp')
        inv_rms = lax.rsqrt(sq_sums / model_dim + EPS_NORM)[:, :, None]
        q_hat = q_raw * inv_rms[0]
        k_hat = k_raw * inv_rms[1]
        q_rot = rope_rotate((q_hat * g_q).reshape(head_shape), cos_bcast, sin_bcast).astype(jnp.bfloat16)
        k_rot = rope_rotate((k_hat * g_k).reshape(head_shape), cos_bcast, sin_bcast).astype(jnp.bfloat16)
        attn_out, attn_pull = jax.vjp(attend, q_rot, k_rot, v_heads)
        o_flat = attn_out.reshape(rows_all, heads_loc * HEAD_DIM)
        part_sum = jnp.dot(o_flat, w_o, preferred_element_type=jnp.float32).astype(jnp.bfloat16).reshape(batch_size, seq_len, model_dim)
        proj_loc = lax.psum_scatter(part_sum, 'tp', scatter_dimension=1, tiled=True).astype(jnp.float32) + b_o
        x_out = (x_float + gate_row * proj_loc).astype(jnp.bfloat16)

        dy_float = dy_loc.astype(jnp.float32)
        d_gate = jnp.sum(dy_float * proj_loc, axis=1)
        d_proj = lax.all_gather((dy_float * gate_row).astype(jnp.bfloat16), 'tp', axis=1, tiled=True).reshape(rows_all, model_dim)
        d_wo = lax.dot_general(o_flat, d_proj, ROW_CONTRACT, preferred_element_type=jnp.float32).astype(jnp.bfloat16)
        d_attn = lax.dot_general(d_proj, w_o, COL_CONTRACT, preferred_element_type=jnp.float32).astype(jnp.bfloat16).reshape(head_shape)
        dq_rot, dk_rot, dv_heads = attn_pull(d_attn)
        dq_hat = rope_rotate(dq_rot.astype(jnp.float32), cos_bcast, -sin_bcast).reshape(rows_all, -1)
        dk_hat = rope_rotate(dk_rot.astype(jnp.float32), cos_bcast, -sin_bcast).reshape(rows_all, -1)
        d_gq = jnp.sum(dq_hat * q_hat, axis=0)
        d_gk = jnp.sum(dk_hat * k_hat, axis=0)
        dq_scaled = dq_hat * g_q
        dk_scaled = dk_hat * g_k
        stat_grads = lax.psum(jnp.stack([jnp.sum(dq_scaled * q_hat, axis=-1), jnp.sum(dk_scaled * k_hat, axis=-1)]), 'tp')[:, :, None] / model_dim
        dq_raw = (inv_rms[0] * (dq_scaled - q_hat * stat_grads[0])).astype(jnp.bfloat16)
        dk_raw = (inv_rms[1] * (dk_scaled - k_hat * stat_grads[1])).astype(jnp.bfloat16)
        dv_flat = dv_heads.reshape(rows_all, -1)
        d_wq = lax.dot_general(y_full, dq_raw, ROW_CONTRACT, preferred_element_type=jnp.float32).astype(jnp.bfloat16)
        d_wk = lax.dot_general(y_full, dk_raw, ROW_CONTRACT, preferred_element_type=jnp.float32).astype(jnp.bfloat16)
        d_wv = lax.dot_general(y_full, dv_flat, ROW_CONTRACT, preferred_element_type=jnp.float32).astype(jnp.bfloat16)
        dy_part = (lax.dot_general(dq_raw, w_q, COL_CONTRACT, preferred_element_type=jnp.float32)
                   + lax.dot_general(dk_raw, w_k, COL_CONTRACT, preferred_element_type=jnp.float32)
                   + lax.dot_general(dv_flat, w_v, COL_CONTRACT, preferred_element_type=jnp.float32))
        dy_part = dy_part.astype(jnp.bfloat16).reshape(batch_size, seq_len, model_dim)
        d_y = lax.psum_scatter(dy_part, 'tp', scatter_dimension=1, tiled=True).astype(jnp.float32)
        d_mod = lax.psum(jnp.stack([jnp.sum(d_y, axis=1), jnp.sum(d_y * x_norm, axis=1), d_gate], axis=1), 'tp')
        d_norm = d_y * scale_one
        d_x = dy_float + inv_std * (d_norm - jnp.mean(d_norm, axis=-1, keepdims=True) - x_norm * jnp.mean(d_norm * x_norm, axis=-1, keepdims=True))
        return (x_out, d_x.astype(jnp.bfloat16), d_mod, jnp.sum(d_mod, axis=0), d_wq, d_wk, d_wv, d_wo, d_gq, d_gk)

    in_specs = (P('dp', 'tp', None), P('dp', None, None), P(None, None), P(None, 'tp'), P('tp'), P(None, 'tp'), P('tp'),
                P(None, 'tp'), P('tp'), P('tp', None), P(None), P('tp'), P('tp'), P('dp', None), P('dp', 'tp', None))
    out_specs = (P('dp', 'tp', None), P('dp', 'tp', None), P('dp', None, None), P('dp', None), P('dp', 'tp'), P('dp', 'tp'),
                 P('dp', 'tp'), P(('dp', 'tp'), None), P(('dp', 'tp')), P(('dp', 'tp')))
    return jax.shard_map(device_step, mesh=mesh, in_specs=in_specs, out_specs=out_specs, check_vma=False)
```

profile of v0, /device:TPU:0, one launch (start us, length us, event | category | flops | bytes accessed | tf_op | source)
XLA Modules:
  0.0 1798.6 jit_solution(12659547897456719282)
XLA Ops:
  33.3 221.1 %all-gather.3.cloned.1.call-done = bf16[16,512,3072]{2,1,0:T(8,128)(2,1)} async-done(((bf16[16,64,3072]{2,1,0:T(8,128)(2,1)}), bf16[16,512,3072]{2,1,0:T(8,128)(2,1)}) %all-gather.3.cloned.1.call-update) | async-done | bytes 50331664 | tf_op jit(solution)/shard_map/all_gather | solution.py:63
  254.5 27.8 %multiply_reduce_fusion.5 = (f32[8192]{0:T(1024)S(1)}, f32[8192,384]{0,1:T(8,128)}) fusion(f32[384]{0:T(512)S(1)} %copy-done.30, bf16[8192,3072]{1,0:T(8,128)(2,1)} %bitcast.140, bf16[3072,384]{1,0:T(8,128)(2,1)S(1)} %copy-done), kind=kOutput, calls=%fused_computation.55 | convolution fusion | flops 19336781824 | bytes 65308160 | tf_op jit(solution)/shard_map/dot_general | solution.py:66
  282.3 29.1 %multiply_reduce_fusion.6 = (f32[8192]{0:T(1024)S(1)}, f32[8192,384]{0,1:T(8,128)}) fusion(f32[384]{0:T(512)S(1)} %copy-done.31, bf16[8192,3072]{1,0:T(8,128)(2,1)} %bitcast.141, bf16[3072,384]{1,0:T(8,128)(2,1)} %param.18), kind=kOutput, calls=%fused_computation.56 | convolution fusion | flops 19336781824 | bytes 65308160 | tf_op jit(solution)/shard_map/dot_general | solution.py:65
  312.1 33.5 %add_convert_fusion.1 = bf16[8192,384]{1,0:T(8,128)(2,1)} fusion(bf16[8192,3072]{1,0:T(8,128)(2,1)} %bitcast.142, bf16[3072,384]{1,0:T(8,128)(2,1)} %param.22, f32[384]{0:T(512)S(1)} %copy-done.32), kind=kOutput, calls=%fused_computation.57 | convolution fusion | flops 19333644288 | bytes 58983936 | tf_op jit(solution)/shard_map/dot_general | solution.py:67
  345.7 139.5 %all-gather.5.cloned.1.call-done = bf16[16,512,3072]{2,1,0:T(8,128)(2,1)} async-done(((bf16[16,64,3072]{2,1,0:T(8,128)(2,1)}), bf16[16,512,3072]{2,1,0:T(8,128)(2,1)}) %all-gather.5.cloned.1.call-update) | async-done | bytes 50331664 | tf_op jit(solution)/shard_map/all_gather | solution.py:82
  485.2 33.4 %convolution_convert_fusion.2 = bf16[8192,384]{1,0:T(8,128)(2,1)} fusion(bf16[8192,3072]{1,0:T(8,128)(2,1)} %bitcast.146, bf16[384,3072]{1,0:T(8,128)(2,1)} %param.24), kind=kOutput, calls=%fused_computation.60 | convolution fusion | flops 19330498560 | bytes 58982400 | tf_op jit(solution)/shard_map/dot_general | solution.py:84
  565.2 21.1 %copy.90 = f32[48,8,16,512]{3,2,1,0:T(8,128)} copy(f32[48,8,16,512]{3,1,2,0:T(8,128)} %bitcast.106) | data formatting | bytes 25165824
  597.9 21.2 %copy.91 = f32[48,8,16,512]{3,2,1,0:T(8,128)} copy(f32[48,8,16,512]{3,1,2,0:T(8,128)} %bitcast.107) | data formatting | bytes 25165824
  637.6 35.2 %fusion.72 = (f32[16,3,512]{2,1,0:T(4,128)S(1)}, f32[16,3,512,512]{2,3,1,0:T(8,128)}) fusion(bf16[16,512,3,128]{1,0,3,2:T(8,128)(2,1)} %bitcast.123, bf16[16,512,3,128]{1,0,3,2:T(8,128)(2,1)} %bitcast.121), kind=kOutput, calls=%fused_computation.126 | convolution fusion | flops 3258974720 | bytes 63012864 | tf_op jit(solution)/shard_map/jvp()/sub | solution.py:37
  672.8 55.8 %fusion.5 = (f32[16,3,512]{2,1,0:T(4,128)S(1)}, bf16[16,3,512,512]{2,3,1,0:T(8,128)(2,1)}, bf16[16,3,512,512]{2,3,1,0:T(8,128)(2,1)}) fusion(f32[16,3,512,512]{2,3,1,0:T(8,128)} %get-tuple-element.49, f32[16,3,512]{2,1,0:T(4,128)S(1)} %multiply_divide_fusion, f32[16,3,512]{2,1,0:T(4,128)S(1)} %get-tuple-element.48, bf16[16,3,128,512]{3,0,2,1:T(8,128)(2,1)} %bitcast.112, ...), kind=kOutput, calls=%fused_computation.8 | convolution fusion | flops 3309281280 | bytes 113541120 | tf_op jit(solution)/shard_map/transpose(jvp(bhqk,bkhd->bqhd))/dot_general | solution.py:38
  728.6 31.9 %convert_bitcast_fusion = f32[16,512,3,128]{1,3,2,0:T(8,128)} fusion(bf16[16,512,3,128]{1,0,3,2:T(8,128)(2,1)} %bitcast.124, f32[16,3,512,512]{2,3,1,0:T(8,128)} %get-tuple-element.49, bf16[16,3,512,512]{2,3,1,0:T(8,128)(2,1)} %get-tuple-element.50, f32[16,3,512]{2,1,0:T(4,128)S(1)} %neg.23, f32[16,3,512]{2,1,0:T(4,128)S(1)} %get-tuple-element.48), kind=kOutput, calls=%fused_computation.46 | convolution fusion | flops 3290431488 | bytes 94568448 | tf_op jit(solution)/shard_map/transpose(jvp(bqhd,bkhd->bhqk))/dot_general | solution.py:36
  760.5 30.7 %convert_bitcast_fusion.1 = f32[16,512,3,128]{1,3,2,0:T(8,128)} fusion(bf16[16,512,3,128]{1,0,3,2:T(8,128)(2,1)S(1)} %bitcast.122, f32[16,3,512,512]{2,3,1,0:T(8,128)} %get-tuple-element.49, bf16[16,3,512,512]{2,3,1,0:T(8,128)(2,1)} %get-tuple-element.50, f32[16,3,512]{2,1,0:T(4,128)S(1)} %neg.23, f32[16,3,512]{2,1,0:T(4,128)S(1)} %get-tuple-element.48), kind=kOutput, calls=%fused_computation.47 | convolution fusion | flops 3290431488 | bytes 94568448 | tf_op jit(solution)/shard_map/transpose(jvp(bqhd,bkhd->bhqk))/dot_general | solution.py:36
  852.5 22.0 %copy.95 = f32[48,8,16,512]{3,1,2,0:T(8,128)} copy(f32[48,8,16,512]{3,2,1,0:T(8,128)} %bitcast.104) | data formatting | bytes 25165824
  897.0 21.8 %copy.94 = f32[48,8,16,512]{3,1,2,0:T(8,128)} copy(f32[48,8,16,512]{3,2,1,0:T(8,128)} %bitcast.105) | data formatting | bytes 25165824
  1001.0 40.8 %fusion.82 = f32[8192,3072]{1,0:T(8,128)} fusion(bf16[8192,384]{0,1:T(8,128)(2,1)} %multiply_convert_fusion, bf16[3072,384]{1,0:T(8,128)(2,1)S(1)} %copy-done), kind=kOutput, calls=%fused_computation.128 | convolution fusion | flops 19327352832 | bytes 109314048 | tf_op jit(solution)/shard_map/dot_general | solution.py:100
  1041.8 41.4 %fusion.81 = f32[8192,3072]{1,0:T(8,128)} fusion(bf16[8192,384]{0,1:T(8,128)(2,1)} %multiply_convert_fusion.1, bf16[3072,384]{1,0:T(8,128)(2,1)} %param.18), kind=kOutput, calls=%fused_computation.127 | convolution fusion | flops 19327352832 | bytes 109314048 | tf_op jit(solution)/shard_map/dot_general | solution.py:99
  1083.2 81.7 %add_convert_fusion = bf16[8192,3072]{1,0:T(8,128)(2,1)} fusion(f32[8192,3072]{1,0:T(8,128)} %fusion.81, f32[8192,3072]{1,0:T(8,128)} %fusion.82, bf16[8192,384]{0,1:T(8,128)(2,1)} %bitcast.114, bf16[3072,384]{1,0:T(8,128)(2,1)S(1)} %copy-done.5), kind=kOutput, calls=%fused_computation.1 | convolution fusion | flops 19402850304 | bytes 260308992 | tf_op jit(solution)/shard_map/dot_general | solution.py:101
  1197.3 35.1 %convolution_convert_fusion = bf16[8192,3072]{1,0:T(8,128)(2,1)} fusion(bf16[8192,384]{0,1:T(8,128)(2,1)} %bitcast.119, bf16[384,3072]{1,0:T(8,128)(2,1)S(1)} %copy-done.29), kind=kOutput, calls=%fused_computation.11 | convolution fusion | flops 19352518656 | bytes 58982400 | tf_op jit(solution)/shard_map/dot_general | solution.py:76
  1232.4 28.7 %convolution_convert_fusion.3 = bf16[384,3072]{1,0:T(8,128)(2,1)} fusion(bf16[8192,384]{0,1:T(8,128)(2,1)} %bitcast.120, bf16[8192,3072]{1,0:T(8,128)(2,1)} %bitcast.147), kind=kOutput, calls=%fused_computation.90 | convolution fusion | flops 19328532480 | bytes 58982400 | tf_op jit(solution)/shard_map/dot_general | solution.py:83
  1261.1 34.2 %convolution_convert_fusion.4 = bf16[3072,384]{1,0:T(8,128)(2,1)} fusion(bf16[8192,3072]{1,0:T(8,128)(2,1)} %bitcast.143, bf16[8192,384]{0,1:T(8,128)(2,1)} %bitcast.115), kind=kOutput, calls=%fused_computation.91 | convolution fusion | flops 19328532480 | bytes 58982400 | tf_op jit(solution)/shard_map/dot_general | solution.py:98
  1295.3 34.4 %convolution_convert_fusion.6 = bf16[3072,384]{1,0:T(8,128)(2,1)} fusion(bf16[8192,3072]{1,0:T(8,128)(2,1)} %bitcast.144, bf16[8192,384]{0,1:T(8,128)(2,1)} %multiply_convert_fusion.1), kind=kOutput, calls=%fused_computation.93 | convolution fusion | flops 19328532480 | bytes 58982400 | tf_op jit(solution)/shard_map/dot_general | solution.py:96
  1329.8 112.0 %reduce-scatter.5.cloned.1.call-done = bf16[16,64,3072]{2,1,0:T(8,128)(2,1)} async-done(((bf16[16,512,3072]{2,1,0:T(8,128)(2,1)}), bf16[16,64,3072]{2,1,0:T(8,128)(2,1)}) %reduce-scatter.5.cloned.1.call-update) | async-done | bytes 6291472 | tf_op jit(solution)/shard_map/reduce_scatter | solution.py:103
  1450.4 272.1 %reduce-scatter.3.cloned.1.call-done = bf16[16,64,3072]{2,1,0:T(8,128)(2,1)} async-done(((bf16[16,512,3072]{2,1,0:T(8,128)(2,1)}), bf16[16,64,3072]{2,1,0:T(8,128)(2,1)}) %reduce-scatter.3.cloned.1.call-update) | async-done | bytes 6291472 | tf_op jit(solution)/shard_map/reduce_scatter | solution.py:77
  1740.5 34.4 %convolution_convert_fusion.5 = bf16[3072,384]{1,0:T(8,128)(2,1)} fusion(bf16[8192,3072]{1,0:T(8,128)(2,1)} %bitcast.145, bf16[8192,384]{0,1:T(8,128)(2,1)} %multiply_convert_fusion), kind=kOutput, calls=%fused_computation.92 | convolution fusion | flops 19328532480 | bytes 58982400 | tf_op jit(solution)/shard_map/dot_general | solution.py:97
  (140 shorter events, 345.1 us)
Async XLA Ops:
  7.2 247.3 %copy-start = (bf16[3072,384]{1,0:T(8,128)(2,1)S(1)}, bf16[3072,384]{1,0:T(8,128)(2,1)}, u32[]{:S(2)}) copy-start(bf16[3072,384]{1,0:T(8,128)(2,1)} %param.20) | copy-start | bytes 7077892
  7.2 247.3 %all-gather.3.cloned.1.call-start = ((), (), s32[]{:S(2)}) async-start(), calls=%async_computation.2 | async-start | bytes 56623104 | tf_op jit(solution)/shard_map/all_gather | solution.py:63
  23.2 231.3 %copy-start.30 = (f32[384]{0:T(512)S(1)}, f32[384]{0:T(512)}, u32[]{:S(2)}) copy-start(f32[384]{0:T(512)} %param.21) | copy-start | bytes 4612
  23.3 461.9 %all-gather.5.cloned.1.call-start = ((), (), s32[]{:S(2)}) async-start(), calls=%async_computation.5 | async-start | bytes 56623104 | tf_op jit(solution)/shard_map/all_gather | solution.py:82
  30.5 522.2 %all-reduce.4.cloned.1.call-start = ((), (), s32[]{:S(2)}) async-start(), calls=%async_computation.3 | async-start | bytes 131072 | tf_op jit(solution)/shard_map/psum | solution.py:68
  254.5 27.8 %copy-start.31 = (f32[384]{0:T(512)S(1)}, f32[384]{0:T(512)}, u32[]{:S(2)}) copy-start(f32[384]{0:T(512)} %param.19) | copy-start | bytes 4612
  282.3 29.8 %copy-start.32 = (f32[384]{0:T(512)S(1)}, f32[384]{0:T(512)}, u32[]{:S(2)}) copy-start(f32[384]{0:T(512)} %param.23) | copy-start | bytes 4612
  345.6 630.0 %all-reduce.6.cloned.1.call-start = ((), (), s32[]{:S(2)}) async-start(), calls=%async_computation.6 | async-start | bytes 131072 | tf_op jit(solution)/shard_map/psum | solution.py:92
  553.7 32.6 %copy-start.16 = (f32[1,8192]{1,0:T(1,128)}, f32[1,8192]{1,0:T(1,128)S(1)}, u32[]{:S(2)}) copy-start(f32[1,8192]{1,0:T(1,128)S(1)} %get-tuple-element.42) | copy-start | bytes 98308
  728.6 31.9 %copy-start.2 = (bf16[16,512,3,64,2]{1,0,4,3,2:T(8,128)(2,1)S(1)}, bf16[16,512,3,64,2]{1,0,4,3,2:T(8,128)(2,1)}, u32[]{:S(2)}) copy-start(bf16[16,512,3,64,2]{1,0,4,3,2:T(8,128)(2,1)} %get-tuple-element.52) | copy-start | bytes 18874372
  852.5 22.0 %copy-start.17 = (f32[1,8192]{1,0:T(1,128)S(1)}, f32[1,8192]{1,0:T(1,128)}, u32[]{:S(2)}) copy-start(f32[1,8192]{1,0:T(1,128)} %copy-done.16) | copy-start | bytes 98308
  852.5 22.0 %copy-start.24 = (f32[384]{0:T(512)S(1)}, f32[384]{0:T(512)}, u32[]{:S(2)}) copy-start(f32[384]{0:T(512)} %param.27) | copy-start | bytes 4612
  897.0 21.8 %copy-start.15 = (f32[1,8192]{1,0:T(1,128)S(1)}, f32[1,8192]{1,0:T(1,128)}, u32[]{:S(2)}) copy-start(f32[1,8192]{1,0:T(1,128)} %copy-done.14) | copy-start | bytes 98308
  897.0 21.8 %copy-start.26 = (f32[384]{0:T(512)S(1)}, f32[384]{0:T(512)}, u32[]{:S(2)}) copy-start(f32[384]{0:T(512)} %param.26) | copy-start | bytes 4612
  929.9 511.9 %reduce-scatter.5.cloned.1.call-start = ((), (), s32[]{:S(2)}) async-start(), calls=%async_computation.7 | async-start | bytes 56623104 | tf_op jit(solution)/shard_map/reduce_scatter | solution.py:103
  1041.8 41.4 %copy-start.5 = (bf16[3072,384]{1,0:T(8,128)(2,1)S(1)}, bf16[3072,384]{1,0:T(8,128)(2,1)}, u32[]{:S(2)}) copy-start(bf16[3072,384]{1,0:T(8,128)(2,1)} %param.22) | copy-start | bytes 7077892
  1164.9 557.5 %reduce-scatter.3.cloned.1.call-start = ((), (), s32[]{:S(2)}) async-start(), calls=%async_computation.4 | async-start | bytes 56623104 | tf_op jit(solution)/shard_map/reduce_scatter | solution.py:77
  1232.4 555.4 %all-reduce.8.cloned.1.call-start = ((), (), s32[]{:S(2)}) async-start(), calls=%async_computation.8 | async-start | bytes 1179648 | tf_op jit(solution)/shard_map/psum | solution.py:104
  1295.3 146.4 %copy-start.4 = (f32[16,3072]{1,0:T(8,128)S(1)}, f32[16,3072]{1,0:T(8,128)}, u32[]{:S(2)}) copy-start(f32[16,3072]{1,0:T(8,128)} %copy-done.3) | copy-start | bytes 589828
  1295.3 146.4 %copy-start.19 = (f32[16,64]{1,0:T(8,128)S(1)}, f32[16,64]{1,0:T(8,128)}, u32[]{:S(2)}) copy-start(f32[16,64]{1,0:T(8,128)} %copy-done.18) | copy-start | bytes 12292
  1295.3 146.4 %copy-start.21 = (f32[16,64]{1,0:T(8,128)S(1)}, f32[16,64]{1,0:T(8,128)}, u32[]{:S(2)}) copy-start(f32[16,64]{1,0:T(8,128)} %copy-done.20) | copy-start | bytes 12292
  1329.8 392.7 %copy-start.7 = (f32[16,3072]{1,0:T(8,128)S(1)}, f32[16,3072]{1,0:T(8,128)}, u32[]{:S(2)}) copy-start(f32[16,3072]{1,0:T(8,128)} %copy-done.6) | copy-start | bytes 589828
  1329.8 392.7 %copy-start.27 = (f32[3072]{0:T(1024)S(1)}, f32[3072]{0:T(1024)}, u32[]{:S(2)}) copy-start(f32[3072]{0:T(1024)} %param.25) | copy-start | bytes 36868
  1740.4 51.1 %copy-start.1 = (bf16[3072,384]{1,0:T(8,128)(2,1)S(1)}, bf16[3072,384]{1,0:T(8,128)(2,1)}, u32[]{:S(2)}) copy-start(bf16[3072,384]{1,0:T(8,128)(2,1)} %param.20) | copy-start | bytes 7077892
  (18 other events, 204.2 us)
Sparse Core Ops, SparseCore 0:
  23.4 231.0 all-gather.2
  256.9 228.2 all-gather.4
  488.3 45.5 all-reduce.3
  930.0 45.5 all-reduce.5
  1165.0 276.6 reduce-scatter.4
  1445.2 277.2 reduce-scatter.2
  1740.6 47.1 all-reduce.7
where the time goes:
time: 1810 us; the launch traced here: 1800 us
  waiting for transfers between devices  769 us (42%)
  matrix products  642 us (35%)
  local copies, waits for them, and re-layouts  190 us (10%)
  other arithmetic  182 us (10%)
    reduce_scatter x1, waiting for transfers between devices, device_step(): lax.psum_scatter(part_sum, 'tp', scatter_dimension=1, tiled=True)  272 us
    all_gather x1, waiting for transfers between devices, device_step(): lax.all_gather(y_loc, 'tp', axis=1, tiled=True).reshape(rows_all, model_dim)  221 us
    all_gather x1, waiting for transfers between devices, device_step(): lax.all_gather((dy_float * gate_row).astype(jnp.bfloat16), 'tp', axis=1,...  140 us
    unnamed x78, local copies, waits for them, and re-layouts  118 us
    reduce_scatter x1, waiting for transfers between devices, device_step(): lax.psum_scatter(dy_part, 'tp', scatter_dimension=1, tiled=True)  112 us
    dot_general x3, matrix products, attend(): jnp.einsum('bhqk,bkhd->bqhd', attn_probs, v_heads, preferred_element_type...  89.4 us
    dot_general x1, matrix products, device_step(): lax.dot_general(dv_flat, w_v, COL_CONTRACT, preferred_element_type=jnp.fl...  81.7 us
    dot_general x2, matrix products, attend(): jnp.einsum('bqhd,bkhd->bhqk', q_rot, k_rot, preferred_element_type=jnp.fl...  62.5 us
  transfers between devices with their start and end apart: 7, of which 6 were waited for; matrix products, arithmetic and copies ran while one was open for 23% of the time, Pallas kernels for 0%

commit v1 on v0

--- a/solution.py
+++ b/solution.py
@@ -1,6 +1,10 @@
+import functools
+
 import jax
 import jax.numpy as jnp
 from jax import lax
+from jax.experimental import pallas as pl
+from jax.experimental.pallas import tpu as pltpu
 from jax.sharding import PartitionSpec as P
 
 HEAD_DIM = 128
@@ -8,6 +12,10 @@
 ROPE_BASE = 10000.0
 ROW_CONTRACT = (((0,), (0,)), ((), ()))
 COL_CONTRACT = (((1,), (1,)), ((), ()))
+MESH = pl.DeviceIdType.MESH
+F32 = jnp.float32
+BF16 = jnp.bfloat16
+LOOKAHEAD = 2
 
 
 def rope_angles(positions):
@@ -38,6 +46,218 @@
     return jnp.einsum('bhqk,bkhd->bqhd', attn_probs, v_heads, preferred_element_type=jnp.float32).astype(jnp.bfloat16)
 
 
+class Peers:
+    def __init__(self):
+        me = lax.axis_index('tp')
+        self.me = me
+        core, col, row = lax.rem(me, 2), lax.rem(me // 2, 2), me // 4
+        self.core, self.col, self.row = core, col, row
+
+        def flip(bits):
+            out = me
+            if bits & 1:
+                out = out + 1 - 2 * core
+            if bits & 2:
+                out = out + 2 - 4 * col
+            if bits & 4:
+                out = out + 4 - 8 * row
+            return out
+
+        self.at = [flip(bits) for bits in range(8)]
+
+
+def entry_barrier(peers, which):
+    barrier = pltpu.get_barrier_semaphore()
+    for bits in which:
+        pl.semaphore_signal(barrier, inc=1, device_id={'tp': peers.at[bits]}, device_id_type=MESH)
+    pl.semaphore_wait(barrier, len(which))
+
+
+def wait_bytes(ref, sem):
+    pltpu.make_async_copy(ref, ref, sem).wait()
+
+
+class RowGather:
+    def __init__(self, peers, src, full, sems):
+        self.peers, self.src, self.full = peers, src, full
+        self.send_sem, self.rx, self.ry, self.rd0, self.rd1, self.rp = sems
+        self.seg = src.shape[1]
+
+    def piece(self, b, t, lo=0, n=None):
+        n = self.seg if n is None else n
+        return self.full.at[b, pl.ds(pl.multiple_of(t * self.seg + lo, 32), n), :]
+
+    def send(self, src, dst, b, sem, bits):
+        pltpu.make_async_remote_copy(src_ref=src, dst_ref=dst, send_sem=self.send_sem.at[b], recv_sem=sem.at[b],
+                                     device_id={'tp': self.peers.at[bits]}, device_id_type=MESH).start()
+
+    def own(self, b):
+        mine = self.piece(b, self.peers.me)
+        self.send(self.src.at[b], mine, b, self.rx, 2)
+        self.send(self.src.at[b], mine, b, self.ry, 4)
+        self.send(self.src.at[b], mine, b, self.rp, 1)
+
+    def direct(self, b):
+        half = self.seg // 2
+        from_x, from_y = self.peers.at[2], self.peers.at[4]
+        wait_bytes(self.piece(b, from_x), self.rx.at[b])
+        first = self.piece(b, from_x, 0, half)
+        self.send(first, first, b, self.rd0, 4)
+        self.send(self.piece(b, from_x), self.piece(b, from_x), b, self.rp, 1)
+        wait_bytes(self.piece(b, from_y), self.ry.at[b])
+        second = self.piece(b, from_y, half, half)
+        self.send(second, second, b, self.rd1, 2)
+        self.send(self.piece(b, from_y), self.piece(b, from_y), b, self.rp, 1)
+
+    def diagonal(self, b):
+        half = self.seg // 2
+        diag = self.peers.at[6]
+        wait_bytes(self.piece(b, diag, 0, half), self.rd0.at[b])
+        wait_bytes(self.piece(b, diag, half, half), self.rd1.at[b])
+        self.send(self.piece(b, diag), self.piece(b, diag), b, self.rp, 1)
+
+    def complete(self, b):
+        wait_bytes(self.full.at[b, pl.ds(0, 4 * self.seg), :], self.rp.at[b])
+
+    def load(self, b, slot, sem):
+        for bits in range(8):
+            t = self.peers.at[bits]
+            src = self.src.at[b] if bits == 0 else self.piece(b, t)
+            pltpu.make_async_copy(src, slot.at[pl.ds(pl.multiple_of(t * self.seg, self.seg), self.seg), :], sem).start()
+
+    def drain(self, b):
+        wait_bytes(self.full.at[b, pl.ds(0, 7 * self.seg), :], self.send_sem.at[b])
+
+
+def project_kernel(y_loc, wq, wk, wv, bias, y_full, qk_out, v_out, st_out,
+                   w_all, slot, qk_stage, v_stage, st_buf,
+                   send_sem, rx, ry, rd0, rd1, rp, w_sem, load_sem, keep_sem, qk_sem, v_sem, st_send, st_recv):
+    peers = Peers()
+    me = peers.me
+    rows, seg, _ = y_loc.shape
+    cols = wq.shape[1]
+    for n, w in enumerate((wq, wk, wv)):
+        pltpu.make_async_copy(w, w_all.at[:, pl.ds(n * cols, cols)], w_sem.at[n]).start()
+    entry_barrier(peers, range(1, 8))
+    gather = RowGather(peers, y_loc, y_full, (send_sem, rx, ry, rd0, rd1, rp))
+    for b in range(LOOKAHEAD):
+        gather.own(b)
+    for n, w in enumerate((wq, wk, wv)):
+        pltpu.make_async_copy(w, w_all.at[:, pl.ds(n * cols, cols)], w_sem.at[n]).wait()
+
+    def keep_copy(b):
+        s = lax.rem(b, 2)
+        return pltpu.make_async_copy(slot.at[s, pl.ds(pl.multiple_of(me * seg, seg), seg), :], gather.piece(b, me), keep_sem.at[s])
+
+    def out_copies(b):
+        s = lax.rem(b, 2)
+        return (pltpu.make_async_copy(qk_stage.at[s], qk_out.at[b], qk_sem.at[s]),
+                pltpu.make_async_copy(v_stage.at[s], v_out.at[b], v_sem.at[s]))
+
+    def send_stats(b):
+        for bits in range(1, 8):
+            pltpu.make_async_remote_copy(src_ref=st_buf.at[me, b], dst_ref=st_buf.at[me, b], send_sem=st_send, recv_sem=st_recv,
+                                         device_id={'tp': peers.at[bits]}, device_id_type=MESH).start()
+
+    def compute(b):
+        s = lax.rem(b, 2)
+        wait_bytes(slot.at[s], load_sem.at[s])
+        keep_copy(b).start()
+
+        @pl.when(b >= 2)
+        def _():
+            for c in out_copies(b - 2):
+                c.wait()
+
+        tile = 256
+        for m in range(slot.shape[1] // tile):
+            block = pl.ds(m * tile, tile)
+            acc = jnp.dot(slot[s, block, :], w_all[...], preferred_element_type=F32) + bias[...]
+            qk_stage[s, block, :] = acc[:, :2 * cols]
+            v_stage[s, block, :] = acc[:, 2 * cols:].astype(BF16)
+        for j in range(slot.shape[1] // 128):
+            for part in range(2):
+                blk = qk_stage[s, pl.ds(j * 128, 128), pl.ds(part * cols, cols)]
+                sq = blk * blk
+                folded = sq[:, :128]
+                for n in range(1, cols // 128):
+                    folded = folded + sq[:, n * 128:(n + 1) * 128]
+                st_buf[me, b, pl.ds(part * 4 + j, 1), :] = jnp.sum(folded.T, axis=0, keepdims=True)
+        for c in out_copies(b):
+            c.start()
+
+    def step(i, carry):
+        @pl.when(i + LOOKAHEAD < rows)
+        def _():
+            gather.own(i + LOOKAHEAD)
+
+        @pl.when(i < rows)
+        def _():
+            gather.direct(i)
+
+        @pl.when((i >= 1) & (i < rows + 1))
+        def _():
+            gather.diagonal(i - 1)
+
+        @pl.when((i >= 2) & (i < rows + 2))
+        def _():
+            b = i - 2
+            gather.complete(b)
+
+            @pl.when(b >= 2)
+            def _():
+                keep_copy(b - 2).wait()
+
+            gather.load(b, slot.at[lax.rem(b, 2)], load_sem.at[lax.rem(b, 2)])
+
+        @pl.when((i >= 3) & (i < rows + 3))
+        def _():
+            compute(i - 3)
+
+        @pl.when(i >= 4)
+        def _():
+            send_stats(i - 4)
+
+        return carry
+
+    lax.fori_loop(0, rows + 4, step, 0)
+    for b in (rows - 2, rows - 1):
+        for c in out_copies(b):
+            c.wait()
+        keep_copy(b).wait()
+
+    def drain(b, carry):
+        gather.drain(b)
+        return carry
+
+    lax.fori_loop(0, rows, drain, 0)
+    wait_bytes(st_buf.at[pl.ds(0, 7)], st_send)
+    wait_bytes(st_buf.at[pl.ds(0, 7)], st_recv)
+    st_out[...] = jnp.sum(st_buf[...], axis=0)
+
+
+def project(y_loc, w_q, w_k, w_v, bias):
+    rows, seg, dim = y_loc.shape
+    cols = w_q.shape[1]
+    seq = seg * 8
+    hbm = pl.BlockSpec(memory_space=pl.ANY)
+    vmem = pl.BlockSpec(memory_space=pltpu.VMEM)
+    dma = pltpu.SemaphoreType.DMA
+    return pl.pallas_call(
+        project_kernel,
+        out_shape=(jax.ShapeDtypeStruct((rows, seq, dim), BF16), jax.ShapeDtypeStruct((rows, seq, 2 * cols), F32),
+                   jax.ShapeDtypeStruct((rows, seq, cols), BF16), jax.ShapeDtypeStruct((rows, 8, 128), F32)),
+        in_specs=[hbm, hbm, hbm, hbm, vmem],
+        out_specs=(hbm, hbm, hbm, vmem),
+        scratch_shapes=[pltpu.VMEM((dim, 3 * cols), BF16), pltpu.VMEM((2, seq, dim), BF16),
+                        pltpu.VMEM((2, seq, 2 * cols), F32), pltpu.VMEM((2, seq, cols), BF16), pltpu.VMEM((8, rows, 8, 128), F32)]
+        + [dma((rows,))] * 6 + [dma((3,)), dma((2,)), dma((2,)), dma((2,)), dma((2,)), dma, dma],
+        compiler_params=pltpu.CompilerParams(collective_id=0, has_side_effects=True, vmem_limit_bytes=60 * 2**20),
+        cost_estimate=pl.CostEstimate(flops=2 * rows * seq * dim * 3 * cols, bytes_accessed=4 * rows * seq * dim, transcendentals=0),
+        name='gather_project',
+    )(y_loc, w_q, w_k, w_v, bias)
+
+
 def solution(mesh):
     tp_size = mesh.shape['tp']
 
@@ -46,6 +266,7 @@
         seq_len = seq_loc * tp_size
         rows_all = batch_size * seq_len
         heads_loc = w_q.shape[1] // HEAD_DIM
+        cols = w_q.shape[1]
         head_shape = (batch_size, seq_len, heads_loc, HEAD_DIM)
         cos_tab, sin_tab = rope_angles(pos_part)
         cos_bcast = cos_tab[None, :, None, :]
@@ -60,12 +281,13 @@
         inv_std = lax.rsqrt(jnp.mean(centered * centered, axis=-1, keepdims=True) + EPS_NORM)
         x_norm = centered * inv_std
         y_loc = (x_norm * scale_one + shift_row).astype(jnp.bfloat16)
-        y_full = lax.all_gather(y_loc, 'tp', axis=1, tiled=True).reshape(rows_all, model_dim)
-
-        q_raw = jnp.dot(y_full, w_q, preferred_element_type=jnp.float32) + b_q
-        k_raw = jnp.dot(y_full, w_k, preferred_element_type=jnp.float32) + b_k
-        v_heads = (jnp.dot(y_full, w_v, preferred_element_type=jnp.float32) + b_v).astype(jnp.bfloat16).reshape(head_shape)
-        sq_sums = lax.psum(jnp.stack([jnp.sum(q_raw * q_raw, axis=-1), jnp.sum(k_raw * k_raw, axis=-1)]), 'tp')
+        y_rows, qk_raw, v_rows, sq_parts = project(y_loc, w_q, w_k, w_v, jnp.concatenate([b_q, b_k, b_v])[None])
+        y_full = y_rows.reshape(rows_all, model_dim)
+        q_raw = qk_raw[:, :, :cols].reshape(rows_all, cols)
+        k_raw = qk_raw[:, :, cols:].reshape(rows_all, cols)
+        v_heads = v_rows.reshape(head_shape)
+        sq_sums = jnp.moveaxis(sq_parts.reshape(batch_size, 2, seq_len), 1, 0).reshape(2, rows_all)
+
         inv_rms = lax.rsqrt(sq_sums / model_dim + EPS_NORM)[:, :, None]
         q_hat = q_raw * inv_rms[0]
         k_hat = k_raw * inv_rms[1]

time: 1810 us -> 1780 us (0.983)
  Pallas kernels: 0 us -> 424 us
  waiting for transfers between devices: 769 us -> 360 us
  matrix products: 642 us -> 546 us
  local copies, waits for them, and re-layouts: 190 us -> 256 us
    pallas_call x0 -> x1, Pallas kernels: none -> 424 us  [project(): pl.pallas_call(project_kernel, out_shape=(jax.ShapeDtypeStruct((rows, seq...]
    all_gather x1 -> x0, waiting for transfers between devices: 221 us -> none  [device_step(): lax.all_gather(y_loc, 'tp', axis=1, tiled=True).reshape(rows_all, model_dim)]
    all_gather x1, waiting for transfers between devices: 140 us -> 0.02 us  [device_step(): lax.all_gather((dy_float * gate_row).astype(jnp.bfloat16), 'tp', axis=1,...]
    dot_general x3 -> x0, matrix products: 90.4 us -> none  [the longest x1 33.5 us: device_step(): jnp.dot(y_full, w_v, preferred_element_type=jnp.float32) + b_v]
    slice x0 -> x3, local copies, waits for them, and re-layouts: none -> 44 us  [the longest x2 31.3 us: device_step(): k_raw = qk_raw[:, :, cols:].reshape(rows_all, cols)]
    reduce_scatter x1, waiting for transfers between devices: 112 us -> 74.3 us  [device_step(): lax.psum_scatter(dy_part, 'tp', scatter_dimension=1, tiled=True)]
    another operation x0 -> x2, local copies, waits for them, and re-layouts: none -> 25.3 us  [rope_rotate(): jnp.stack([even_part * cos_part - odd_part * sin_part, even_part * sin_pa...]
    unnamed x78 -> x87, local copies, waits for them, and re-layouts: 118 us -> 96.5 us
  transfers between devices with their start and end apart: 7 -> 5, of which waited for: 6 -> 3; matrix products, arithmetic and copies ran while one was open for 23% -> 28% of each run, Pallas kernels for 0% -> 24%
where the time goes in v1:
time: 1780 us
  matrix products  546 us (31%)
  Pallas kernels  424 us (24%)
  waiting for transfers between devices  360 us (20%)
  local copies, waits for them, and re-layouts  256 us (14%)
  other arithmetic  175 us (10%)
    pallas_call x1, Pallas kernels, project(): pl.pallas_call(project_kernel, out_shape=(jax.ShapeDtypeStruct((rows, seq...  424 us
    reduce_scatter x1, waiting for transfers between devices, device_step(): lax.psum_scatter(part_sum, 'tp', scatter_dimension=1, tiled=True)  272 us
    unnamed x87, local copies, waits for them, and re-layouts  96.5 us
    dot_general x1, matrix products, device_step(): lax.dot_general(dv_flat, w_v, COL_CONTRACT, preferred_element_type=jnp.fl...  83.4 us
    reduce_scatter x1, waiting for transfers between devices, device_step(): lax.psum_scatter(dy_part, 'tp', scatter_dimension=1, tiled=True)  74.3 us
    dot_general x3, matrix products, attend(): jnp.einsum('bhqk,bkhd->bqhd', attn_probs, v_heads, preferred_element_type...  70 us
    dot_general x2, matrix products, attend(): jnp.einsum('bqhd,bkhd->bhqk', q_rot, k_rot, preferred_element_type=jnp.fl...  63.5 us
    dot_general x1, matrix products, device_step(): lax.dot_general(dq_raw, w_q, COL_CONTRACT, preferred_element_type=jnp.flo...  47 us
  transfers between devices with their start and end apart: 5, of which 3 were waited for; matrix products, arithmetic and copies ran while one was open for 28% of the time, Pallas kernels for 24%

profile of v1, /device:TPU:0, one launch (start us, length us, event | category | flops | bytes accessed | tf_op | source)
XLA Modules:
  0.0 1776.0 jit_solution(11039358843716310896)
XLA Ops:
  37.0 424.4 %gather_project.1 = (bf16[16,512,3072]{2,1,0:T(8,128)(2,1)}, f32[16,512,768]{2,1,0:T(8,128)}, bf16[16,512,384]{2,1,0:T(8,128)(2,1)}, f32[16,8,128]{2,1,0:T(8,128)}) custom-call(bf16[16,64,3072]{2,1,0:T(8,128)(2,1)} %fusion.20.y_loc, bf16[3072,384]{1,0:T(8,128)(2,1)} %wq.1, bf16[3072,384]{1,0:T(8,128)(2,1)} %wk.1, bf16[3072,384]{1,0:T(8,128)(2,1)} %wv.1, ...), custom_call_target="tpu_custom_call" | custom-call | flops 57982058496 | bytes 100663296 | tf_op jit(solution)/shard_map/gather_project/pallas_call | solution.py:246
  470.1 18.6 %fusion.72 = (f32[16,512,384]{2,1,0:T(8,128)}, f32[16,512,384]{2,1,0:T(8,128)}) fusion(f32[16,512,768]{2,1,0:T(8,128)} %get-tuple-element.15), kind=kLoop, calls=%fused_computation.129 | loop fusion | bytes 50331648 | tf_op jit(solution)/shard_map/slice | solution.py:287
  580.7 35.0 %fusion.75 = (f32[16,3,512]{2,1,0:T(4,128)S(1)}, f32[16,3,512,512]{2,3,1,0:T(8,128)}) fusion(bf16[16,512,3,128]{1,0,3,2:T(8,128)(2,1)} %bitcast.135, bf16[16,512,3,128]{1,0,3,2:T(8,128)(2,1)} %bitcast.133), kind=kOutput, calls=%fused_computation.132 | convolution fusion | flops 3258974720 | bytes 63012864 | tf_op jit(solution)/shard_map/jvp()/sub | solution.py:45
  615.8 33.1 %convolution_convert_fusion.2 = bf16[8192,384]{1,0:T(8,128)(2,1)} fusion(bf16[8192,3072]{1,0:T(8,128)(2,1)} %bitcast.152, bf16[384,3072]{1,0:T(8,128)(2,1)S(1)} %copy-done), kind=kOutput, calls=%fused_computation.59 | convolution fusion | flops 19330498560 | bytes 58982400 | tf_op jit(solution)/shard_map/dot_general | solution.py:306
  665.8 37.2 %fusion.5 = (f32[16,3,512]{2,1,0:T(4,128)S(1)}, bf16[16,3,512,512]{2,3,1,0:T(8,128)(2,1)}, bf16[16,3,512,512]{2,3,1,0:T(8,128)(2,1)}) fusion(f32[16,3,512,512]{2,3,1,0:T(8,128)} %get-tuple-element.59, f32[16,3,512]{2,1,0:T(4,128)S(1)} %multiply_divide_fusion, f32[16,3,512]{2,1,0:T(4,128)S(1)} %get-tuple-element.58, bf16[16,512,3,128]{1,3,2,0:T(8,128)(2,1)} %bitcast.121, ...), kind=kOutput, calls=%fused_computation.8 | convolution fusion | flops 3309281280 | bytes 113541120 | tf_op jit(solution)/shard_map/transpose(jvp(bhqk,bkhd->bqhd))/dot_general | solution.py:46
  703.1 31.9 %convert_bitcast_fusion = f32[16,512,3,128]{1,3,2,0:T(8,128)} fusion(bf16[16,512,3,128]{1,0,3,2:T(8,128)(2,1)} %bitcast.136, f32[16,3,512,512]{2,3,1,0:T(8,128)} %get-tuple-element.59, bf16[16,3,512,512]{2,3,1,0:T(8,128)(2,1)} %get-tuple-element.60, f32[16,3,512]{2,1,0:T(4,128)S(1)} %neg.23, f32[16,3,512]{2,1,0:T(4,128)S(1)} %get-tuple-element.58), kind=kOutput, calls=%fused_computation.46 | convolution fusion | flops 3290431488 | bytes 94568448 | tf_op jit(solution)/shard_map/transpose(jvp(bqhd,bkhd->bhqk))/dot_general | solution.py:44
  734.9 31.6 %convert_bitcast_fusion.1 = f32[16,512,3,128]{1,3,2,0:T(8,128)} fusion(bf16[16,512,3,128]{1,0,3,2:T(8,128)(2,1)} %bitcast.134, f32[16,3,512,512]{2,3,1,0:T(8,128)} %get-tuple-element.59, bf16[16,3,512,512]{2,3,1,0:T(8,128)(2,1)} %get-tuple-element.60, f32[16,3,512]{2,1,0:T(4,128)S(1)} %neg.23, f32[16,3,512]{2,1,0:T(4,128)S(1)} %get-tuple-element.58), kind=kOutput, calls=%fused_computation.47 | convolution fusion | flops 3290431488 | bytes 94568448 | tf_op jit(solution)/shard_map/transpose(jvp(bqhd,bkhd->bhqk))/dot_general | solution.py:44
  766.6 16.3 copy.101
  782.9 16.8 copy.102
  865.3 18.2 %multiply_reduce_fusion.1 = (f32[384]{0:T(512)}, f32[16,512]{1,0:T(8,128)S(1)}, f32[16,512]{1,0:T(8,128)S(1)}, f32[384]{0:T(512)}) fusion(f32[16,512,384]{2,1,0:T(8,128)} %copy.89, f32[16,512]{1,0:T(8,128)S(1)} %copy-done.20, f32[16,512,768]{2,1,0:T(8,128)} %get-tuple-element.15, f32[384]{0:T(512)S(1)} %copy-done.29, f32[16,512]{1,0:T(8,128)S(1)} %copy-done.17, ...), kind=kLoop, calls=%fused_computation.48 | loop fusion | flops 37731584 | bytes 50468864 | tf_op jit(solution)/shard_map/reduce_sum | solution.py:311
  884.3 18.0 %convert_bitcast_fusion.2 = bf16[16,512,3,128]{1,3,2,0:T(8,128)(2,1)} fusion(bf16[16,3,512,512]{2,3,1,0:T(8,128)(2,1)} %get-tuple-element.31, bf16[16,3,128,512]{3,0,2,1:T(8,128)(2,1)} %bitcast.124), kind=kOutput, calls=%fused_computation.64 | convolution fusion | flops 3224371200 | bytes 37748736 | tf_op jit(solution)/shard_map/transpose(jvp(bhqk,bkhd->bqhd))/dot_general | solution.py:46
  918.8 21.8 %copy.107 = f32[48,8,16,512]{3,1,2,0:T(8,128)} copy(f32[48,8,16,512]{3,2,1,0:T(8,128)} %bitcast.111) | data formatting | bytes 25165824
  940.6 22.2 %copy.110 = f32[48,8,16,512]{3,1,2,0:T(8,128)} copy(f32[48,8,16,512]{3,2,1,0:T(8,128)} %bitcast.113) | data formatting | bytes 25165824
  964.6 47.0 %fusion.31 = f32[8192,3072]{1,0:T(8,128)} fusion(bf16[3072,384]{1,0:T(8,128)(2,1)} %wk.1, f32[8192,384]{0,1:T(8,128)} %copy.90, f32[8192,384]{0,1:T(8,128)} %bitcast.117, f32[8192]{0:T(1024)S(1)} %bitcast.146, f32[384]{0:T(512)S(1)} %copy-done.29, f32[8192]{0:T(1024)S(1)} %bitcast.144), kind=kOutput, calls=%fused_computation.61 | convolution fusion | flops 19346227200 | bytes 128255488 | tf_op jit(solution)/shard_map/dot_general | solution.py:322
  1011.6 47.0 %fusion.30 = f32[8192,3072]{1,0:T(8,128)} fusion(bf16[3072,384]{1,0:T(8,128)(2,1)} %wq.1, f32[8192,384]{0,1:T(8,128)} %copy.83, f32[8192,384]{0,1:T(8,128)} %bitcast.116, f32[8192]{0:T(1024)S(1)} %bitcast.145, f32[384]{0:T(512)S(1)} %copy-done.31, f32[8192]{0:T(1024)S(1)} %bitcast.143), kind=kOutput, calls=%fused_computation.60 | convolution fusion | flops 19346227200 | bytes 128255488 | tf_op jit(solution)/shard_map/dot_general | solution.py:321
  1058.6 83.4 %add_convert_fusion = bf16[8192,3072]{1,0:T(8,128)(2,1)} fusion(f32[8192,3072]{1,0:T(8,128)} %fusion.30, f32[8192,3072]{1,0:T(8,128)} %fusion.31, bf16[8192,384]{0,1:T(8,128)(2,1)} %bitcast.125, bf16[3072,384]{1,0:T(8,128)(2,1)} %wv.1), kind=kOutput, calls=%fused_computation.1 | convolution fusion | flops 19402850304 | bytes 260308992 | tf_op jit(solution)/shard_map/dot_general | solution.py:323
  1173.4 35.1 %convolution_convert_fusion = bf16[8192,3072]{1,0:T(8,128)(2,1)} fusion(bf16[8192,384]{0,1:T(8,128)(2,1)} %bitcast.137, bf16[384,3072]{1,0:T(8,128)(2,1)S(1)} %copy-done), kind=kOutput, calls=%fused_computation.11 | convolution fusion | flops 19352518656 | bytes 58982400 | tf_op jit(solution)/shard_map/dot_general | solution.py:298
  1208.5 28.6 %convolution_convert_fusion.3 = bf16[384,3072]{1,0:T(8,128)(2,1)} fusion(bf16[8192,384]{0,1:T(8,128)(2,1)} %bitcast.138, bf16[8192,3072]{1,0:T(8,128)(2,1)} %bitcast.153), kind=kOutput, calls=%fused_computation.92 | convolution fusion | flops 19328532480 | bytes 58982400 | tf_op jit(solution)/shard_map/dot_general | solution.py:305
  1237.1 34.2 %convolution_convert_fusion.4 = bf16[3072,384]{1,0:T(8,128)(2,1)} fusion(bf16[8192,3072]{1,0:T(8,128)(2,1)} %bitcast.154, bf16[8192,384]{0,1:T(8,128)(2,1)} %bitcast.126), kind=kOutput, calls=%fused_computation.93 | convolution fusion | flops 19328532480 | bytes 58982400 | tf_op jit(solution)/shard_map/dot_general | solution.py:320
  1310.7 34.4 %convolution_convert_fusion.5 = bf16[3072,384]{1,0:T(8,128)(2,1)} fusion(bf16[8192,3072]{1,0:T(8,128)(2,1)} %bitcast.155, bf16[8192,384]{0,1:T(8,128)(2,1)} %bitcast.139), kind=kOutput, calls=%fused_computation.94 | convolution fusion | flops 19328532480 | bytes 58982400 | tf_op jit(solution)/shard_map/dot_general | solution.py:319
  1345.1 74.3 %reduce-scatter.5.cloned.1.call-done = bf16[16,64,3072]{2,1,0:T(8,128)(2,1)} async-done(((bf16[16,512,3072]{2,1,0:T(8,128)(2,1)}), bf16[16,64,3072]{2,1,0:T(8,128)(2,1)}) %reduce-scatter.5.cloned.1.call-update) | async-done | bytes 6291472 | tf_op jit(solution)/shard_map/reduce_scatter | solution.py:325
  1428.1 272.1 %reduce-scatter.3.cloned.1.call-done = bf16[16,64,3072]{2,1,0:T(8,128)(2,1)} async-done(((bf16[16,512,3072]{2,1,0:T(8,128)(2,1)}), bf16[16,64,3072]{2,1,0:T(8,128)(2,1)}) %reduce-scatter.3.cloned.1.call-update) | async-done | bytes 6291472 | tf_op jit(solution)/shard_map/reduce_scatter | solution.py:299
  1700.2 17.1 fusion.28
  1718.2 34.4 %convolution_convert_fusion.6 = bf16[3072,384]{1,0:T(8,128)(2,1)} fusion(bf16[8192,3072]{1,0:T(8,128)(2,1)} %bitcast.156, bf16[8192,384]{0,1:T(8,128)(2,1)} %bitcast.132), kind=kOutput, calls=%fused_computation.95 | convolution fusion | flops 19328532480 | bytes 58982400 | tf_op jit(solution)/shard_map/dot_general | solution.py:318
  (153 shorter events, 328.7 us)
Async XLA Ops:
  7.2 608.6 %copy-start = (bf16[384,3072]{1,0:T(8,128)(2,1)S(1)}, bf16[384,3072]{1,0:T(8,128)(2,1)}, u32[]{:S(2)}) copy-start(bf16[384,3072]{1,0:T(8,128)(2,1)} %param.24) | copy-start | bytes 7077892
  7.3 608.5 %all-gather.2.cloned.1.call-start = ((), (), s32[]{:S(2)}) async-start(), calls=%async_computation.3 | async-start | bytes 56623104 | tf_op jit(solution)/shard_map/all_gather | solution.py:304
  8.6 18.5 %copy-start.1 = (f32[16,3072]{1,0:T(8,128)}, f32[16,3072]{1,0:T(8,128)S(1)}, u32[]{:S(2)}) copy-start(f32[16,3072]{1,0:T(8,128)S(1)} %get-tuple-element.47) | copy-start | bytes 589828
  16.5 946.4 %all-reduce.3.cloned.1.call-start = ((), (), s32[]{:S(2)}) async-start(), calls=%async_computation.4 | async-start | bytes 131072 | tf_op jit(solution)/shard_map/psum | solution.py:314
  17.3 532.7 %copy-start.7 = (f32[3,64,2]{2,1,0:T(8,128)}, f32[3,64,2]{2,1,0:T(8,128)S(1)}, u32[]{:S(2)}) copy-start(f32[3,64,2]{2,1,0:T(8,128)S(1)} %mul.464) | copy-start | bytes 4612
  17.5 522.4 %copy-start.9 = (f32[3,64,2]{2,1,0:T(8,128)}, f32[3,64,2]{2,1,0:T(8,128)S(1)}, u32[]{:S(2)}) copy-start(f32[3,64,2]{2,1,0:T(8,128)S(1)} %mul.479) | copy-start | bytes 4612
  18.1 542.0 %copy-start.5 = (f32[512,64]{0,1:T(8,128)}, f32[512,64]{0,1:T(8,128)S(1)}, u32[]{:S(2)}) copy-start(f32[512,64]{0,1:T(8,128)S(1)} %get-tuple-element.52) | copy-start | bytes 393220
  782.9 16.8 copy-start.6
  782.9 16.8 copy-start.15
  852.6 12.7 copy-start.29
  852.6 12.7 copy-start.31
  884.3 535.2 %reduce-scatter.5.cloned.1.call-start = ((), (), s32[]{:S(2)}) async-start(), calls=%async_computation.5 | async-start | bytes 56623104 | tf_op jit(solution)/shard_map/reduce_scatter | solution.py:325
  940.6 23.9 %copy-start.14 = (f32[1,16,512]{2,0,1:T(1,128)S(1)}, f32[1,16,512]{2,0,1:T(1,128)}, u32[]{:S(2)}) copy-start(f32[1,16,512]{2,0,1:T(1,128)} %copy-done.13) | copy-start | bytes 98308
  964.6 47.0 %copy-start.12 = (f32[1,16,512]{2,0,1:T(1,128)S(1)}, f32[1,16,512]{2,0,1:T(1,128)}, u32[]{:S(2)}) copy-start(f32[1,16,512]{2,0,1:T(1,128)} %copy-done.11) | copy-start | bytes 98308
  1142.1 558.1 %reduce-scatter.3.cloned.1.call-start = ((), (), s32[]{:S(2)}) async-start(), calls=%async_computation.2 | async-start | bytes 56623104 | tf_op jit(solution)/shard_map/reduce_scatter | solution.py:299
  1208.5 557.1 %all-reduce.5.cloned.1.call-start = ((), (), s32[]{:S(2)}) async-start(), calls=%async_computation.6 | async-start | bytes 1179648 | tf_op jit(solution)/shard_map/psum | solution.py:326
  1237.1 34.2 %copy-start.27 = (f32[8192]{0:T(1024)S(1)}, f32[8192]{0:T(1024)}, u32[]{:S(2)}) copy-start(f32[8192]{0:T(1024)} %get-tuple-element.28) | copy-start | bytes 98308
  1237.1 34.3 %copy-start.10 = (f32[3,64,2]{2,1,0:T(8,128)S(1)}, f32[3,64,2]{2,1,0:T(8,128)}, u32[]{:S(2)}) copy-start(f32[3,64,2]{2,1,0:T(8,128)} %copy-done.9) | copy-start | bytes 4612
  1237.1 34.3 %copy-start.21 = (f32[16,512]{1,0:T(8,128)S(1)}, f32[16,512]{1,0:T(8,128)}, u32[]{:S(2)}) copy-start(f32[16,512]{1,0:T(8,128)} %copy-done.19) | copy-start | bytes 98308
  1310.7 108.8 %copy-start.2 = (f32[16,3072]{1,0:T(8,128)S(1)}, f32[16,3072]{1,0:T(8,128)}, u32[]{:S(2)}) copy-start(f32[16,3072]{1,0:T(8,128)} %copy-done.1) | copy-start | bytes 589828
  1310.7 108.8 %copy-start.23 = (f32[16,64]{1,0:T(8,128)S(1)}, f32[16,64]{1,0:T(8,128)}, u32[]{:S(2)}) copy-start(f32[16,64]{1,0:T(8,128)} %copy-done.22) | copy-start | bytes 12292
  1310.7 108.8 %copy-start.25 = (f32[16,64]{1,0:T(8,128)S(1)}, f32[16,64]{1,0:T(8,128)}, u32[]{:S(2)}) copy-start(f32[16,64]{1,0:T(8,128)} %copy-done.24) | copy-start | bytes 12292
  1345.1 355.1 %copy-start.4 = (f32[16,3072]{1,0:T(8,128)S(1)}, f32[16,3072]{1,0:T(8,128)}, u32[]{:S(2)}) copy-start(f32[16,3072]{1,0:T(8,128)} %copy-done.3) | copy-start | bytes 589828
  1345.1 355.1 %copy-start.33 = (f32[3072]{0:T(1024)S(1)}, f32[3072]{0:T(1024)}, u32[]{:S(2)}) copy-start(f32[3072]{0:T(1024)} %param.25) | copy-start | bytes 36868
  (19 other events, 149.8 us)
Sparse Core Ops, SparseCore 0:
  16.6 429.0 all-gather.1
  884.4 45.5 all-reduce.2
  1142.2 277.2 reduce-scatter.4
  1422.9 277.2 reduce-scatter.2
  1718.3 47.2 all-reduce.4

commit v2 on v0

v2 whole, which is shorter than its diff:
```python
import functools

import jax
import jax.numpy as jnp
from jax import lax
from jax.experimental import pallas as pl
from jax.experimental.pallas import tpu as pltpu
from jax.sharding import PartitionSpec as P

HEAD_DIM = 128
EPS_NORM = 1e-6
ROPE_BASE = 10000.0
ROW_CONTRACT = (((0,), (0,)), ((), ()))
COL_CONTRACT = (((1,), (1,)), ((), ()))
MESH = pl.DeviceIdType.MESH
F32 = jnp.float32
BF16 = jnp.bfloat16
PARTS = 8
PANEL = 1024
EARLY = 12
VMEM_ALL = 67043328
SCORE_SCALE = HEAD_DIM ** -0.5 * 1.4426950408889634


def rope_angles(positions):
    half_dim = HEAD_DIM // 2
    side_len = HEAD_DIM // 6
    first_len = half_dim - 2 * side_len
    pair_idx = jnp.arange(half_dim)
    section = (pair_idx >= first_len).astype(jnp.int32) + (pair_idx >= first_len + side_len).astype(jnp.int32)
    offset = jnp.where(section == 0, 0, jnp.where(section == 1, first_len, first_len + side_len))
    sec_width = jnp.where(section == 0, first_len, side_len)
    freq_vals = ROPE_BASE ** (-(pair_idx - offset).astype(jnp.float32) / sec_width.astype(jnp.float32))
    select = jnp.where(section[None, :] == jnp.arange(3)[:, None], freq_vals[None, :], 0.0)
    angles = jnp.sum(positions.astype(jnp.float32)[:, :, None] * select[None, :, :], axis=1)
    return jnp.cos(angles), jnp.sin(angles)


def rope_tables(positions):
    cos_tab, sin_tab = (jnp.repeat(t, 2, axis=1) for t in rope_angles(positions))
    even = (jnp.arange(HEAD_DIM) % 2 == 0)[None]
    up = jnp.where(even, -sin_tab, 0.0)
    down = jnp.where(even, 0.0, sin_tab)
    scale = HEAD_DIM ** -0.5
    return jnp.stack([cos_tab, up, down, cos_tab * scale, -up * scale, -down * scale])


class Peers:
    def __init__(self):
        me = lax.axis_index('tp')
        self.me = me
        core, col, row = lax.rem(me, 2), lax.rem(me // 2, 2), me // 4

        def flip(bits):
            out = me
            if bits & 1:
                out = out + 1 - 2 * core
            if bits & 2:
                out = out + 2 - 4 * col
            if bits & 4:
                out = out + 4 - 8 * row
            return out

        self.at = [flip(bits) for bits in range(PARTS)]
        self.partner, self.x, self.y, self.diag = (self.at[bits] for bits in (1, 2, 4, 6))


def entry_barrier(peers, which):
    barrier = pltpu.get_barrier_semaphore()
    for bits in which:
        pl.semaphore_signal(barrier, inc=1, device_id={'tp': peers.at[bits]}, device_id_type=MESH)
    pl.semaphore_wait(barrier, len(which))


def wait_local(ref, sem):
    pltpu.make_async_copy(ref, ref, sem).wait()


def wait_bytes(ref, sem):
    pltpu.make_async_copy(ref, ref, sem).wait()


def even(b):
    return lax.rem(b, 2)


class RowGather:
    def __init__(self, peers, src, full, sems, seg):
        self.peers, self.src, self.full, self.seg = peers, src, full, seg
        self.send_sem, self.rx, self.ry, self.rd0, self.rd1, self.rp = sems
        self.lower, self.upper = (0, seg // 2), (seg // 2, seg // 2)

    def piece(self, b, t, part=None):
        lo, n = part or (0, self.seg)
        return self.full.at[b, pl.ds(pl.multiple_of(t * self.seg + lo, 32), n), :]

    def first(self, b, pieces):
        return self.full.at[b, pl.ds(0, pieces * self.seg), :]

    def send(self, src, dst, b, sem, t):
        pltpu.make_async_remote_copy(src_ref=src, dst_ref=dst, send_sem=self.send_sem.at[b], recv_sem=sem.at[b],
                                     device_id={'tp': t}, device_id_type=MESH).start()

    def own(self, b):
        p = self.peers
        for sem, t in ((self.rx, p.x), (self.ry, p.y), (self.rp, p.partner)):
            self.send(self.src(b), self.piece(b, p.me), b, sem, t)

    def direct(self, b):
        p = self.peers
        for near, sem, part, diag_sem, far in ((p.x, self.rx, self.lower, self.rd0, p.y), (p.y, self.ry, self.upper, self.rd1, p.x)):
            whole, some = self.piece(b, near), self.piece(b, near, part)
            wait_bytes(whole, sem.at[b])
            self.send(some, some, b, diag_sem, far)
            self.send(whole, whole, b, self.rp, p.partner)

    def diagonal(self, b):
        p = self.peers
        wait_bytes(self.piece(b, p.diag, self.lower), self.rd0.at[b])
        wait_bytes(self.piece(b, p.diag, self.upper), self.rd1.at[b])
        self.send(self.piece(b, p.diag), self.piece(b, p.diag), b, self.rp, p.partner)

    def complete(self, b):
        wait_bytes(self.first(b, 4), self.rp.at[b])

    def load(self, b, slot, sem):
        for n, t in enumerate(self.peers.at):
            src = self.piece(b, t) if n else self.src(b)
            pltpu.make_async_copy(src, slot.at[pl.ds(pl.multiple_of(t * self.seg, self.seg), self.seg), :], sem).start()

    def drain(self, b):
        wait_bytes(self.first(b, PARTS - 1), self.send_sem.at[b])


def stage_of(i, lag, count, work):
    @pl.when((i >= lag) & (i < count + lag))
    def _():
        work(i - lag)


def attend_kernel(y_loc, dp_loc, wq, wk, wv, bias, gains, tabs, wo,
                  y_full, dp_full, dqkv_out, o_tok, wo_full, dwo_out, pair_in, pair_out, half_out, dg_out,
                  w_all, y_slot, d_slot, qk_ring, v_ring, rot, o_stage, datt, dqk, dqs, dqkv_stage, col_inv, p_buf, ds_buf,
                  dwo_acc, stage, pair_stage, pair_buf, norm_buf, stat_buf,
                  y_sems, d_sems, wo_sems, w_sem, y_sem, d_sem, keep_sem, norm_send, norm_recv, stat_send, stat_recv,
                  o_send, o_keep, o_recv, out_sem, pair_send, pair_recv, pair_load, pair_sem, wo_keep, z_send, z_recv, dwo_sem, half_send, half_recv):
    peers = Peers()
    me = peers.me
    depth = lax.axis_index('dp')
    rows, seg, dim = y_loc.shape
    seq = seg * PARTS
    cols = wq.shape[1]
    heads = cols // HEAD_DIM
    blk = HEAD_DIM
    blocks = seq // blk
    wide = 2 * cols
    hemi = dim // 2
    weights = [pltpu.make_async_copy(w, w_all.at[:, pl.ds(n * cols, cols)], w_sem.at[n]) for n, w in enumerate((wq, wk, wv))]
    for c in weights:
        c.start()
    barrier = pltpu.get_barrier_semaphore()
    for t in peers.at[1:]:
        pl.semaphore_signal(barrier, inc=1, device_id={'tp': t}, device_id_type=MESH)
    pl.semaphore_signal(barrier, inc=1, device_id={'dp': 1 - depth}, device_id_type=MESH)
    pl.semaphore_wait(barrier, PARTS)
    gy = RowGather(peers, lambda b: y_loc.at[b], y_full, y_sems, seg)
    gd = RowGather(peers, lambda b: dp_loc.at[b], dp_full, d_sems, seg)
    gw = RowGather(peers, lambda b: wo.at[:, pl.ds(pl.multiple_of(b * hemi, HEAD_DIM), hemi)], wo_full, wo_sems, cols)
    gy.own(0)
    gd.own(0)
    gy.own(1)
    dwo_acc[...] = jnp.zeros_like(dwo_acc)
    dg_out[...] = jnp.zeros_like(dg_out)
    for c in weights:
        c.wait()

    def mine(b, width):
        return pl.ds(pl.multiple_of(b * width, width), width)

    keep_y = pltpu.make_async_copy(y_slot.at[mine(me, seg), :], gy.piece(0, me), keep_sem)

    def out_copy(b):
        return pltpu.make_async_copy(dqkv_stage.at[even(b)], dqkv_out.at[b], out_sem.at[even(b)])

    def pair_copy(b):
        return pltpu.make_async_copy(pair_stage.at[even(b)], pair_out.at[b], pair_sem.at[even(b)])

    def o_rows(b, t):
        return o_stage.at[even(b), mine(t, seg), :]

    def keep_o(b):
        return pltpu.make_async_copy(o_rows(b, me), o_tok.at[b, :, mine(me, cols)], o_keep.at[even(b)])

    def keep_wo(h):
        return pltpu.make_async_copy(gw.src(h), wo_full.at[h, mine(me, cols), :], wo_keep.at[h])

    def remote(src, dst, send, recv, device):
        return pltpu.make_async_remote_copy(src_ref=src, dst_ref=dst, send_sem=send, recv_sem=recv, device_id=device, device_id_type=MESH)

    def send_sums(b, buf, send, recv):
        for t in peers.at[1:]:
            remote(buf.at[me, b], buf.at[me, b], send, recv.at[b], {'tp': t}).start()

    def send_row(b):
        send_sums(b, stat_buf, stat_send, stat_recv)
        for t in peers.at[1:]:
            remote(o_rows(b, t), o_tok.at[b, :, mine(me, cols)], o_send.at[even(b)], o_recv, {'tp': t}).start()
        keep_o(b).start()

    def wait_row_sent(b):
        wait_bytes(o_stage.at[even(b), pl.ds(0, seq - seg), :], o_send.at[even(b)])
        keep_o(b).wait()

    def pair_sends(b):
        for n in range(4):
            t = peers.at[1 ^ (2 * n)]
            remote(stage.at[mine(t, seg), :], pair_in.at[b, n], pair_send, pair_recv.at[b], {'tp': peers.at[1]}).start()

    def spread(row):
        return jnp.broadcast_to(row, (blk, blk)).T

    def turned(x, sl, kind):
        c, up, down = tabs[kind, sl, :], tabs[kind + 1, sl, :], tabs[kind + 2, sl, :]
        return x * c + pltpu.roll(x, HEAD_DIM - 1, 1) * up + pltpu.roll(x, 1, 1) * down

    def lane_cols(part, h):
        return pl.ds(part * cols + h * HEAD_DIM, HEAD_DIM)

    def load_y(b):
        gy.complete(b)

        @pl.when(b >= 1)
        def _():
            keep_y.wait()

        gy.load(b, y_slot, y_sem)

    def load_d(b):
        gd.complete(b)
        gd.load(b, d_slot.at[even(b)], d_sem.at[even(b)])

    def qkv(b):
        ring = lax.rem(b, 4)
        wait_local(y_slot, y_sem)
        pltpu.make_async_copy(y_slot.at[mine(me, seg), :], gy.piece(b, me), keep_sem).start()
        tile = 2 * blk
        for m in range(seq // tile):
            sl = pl.ds(m * tile, tile)
            acc = jnp.dot(y_slot[sl, :], w_all[...], preferred_element_type=F32) + bias[...]
            qk_ring[ring, sl, :] = acc[:, :wide]
            v_ring[even(b), sl, :] = acc[:, wide:].astype(BF16)
        for j in range(blocks):
            for part in range(2):
                total = None
                for h in range(heads):
                    x = qk_ring[ring, pl.ds(j * blk, blk), lane_cols(part, h)]
                    total = x * x if total is None else total + x * x
                norm_buf[me, b, pl.ds(part * blocks + j, 1), :] = jnp.sum(total.T, axis=0, keepdims=True)

    def inv_norms(b):
        return lax.rsqrt(jnp.sum(norm_buf[:, b], axis=0) * (1.0 / dim) + EPS_NORM)

    def attend(b):
        s, ring = even(b), lax.rem(b, 4)
        wait_bytes(norm_buf.at[pl.ds(0, PARTS - 1), b], norm_recv.at[b])
        wait_local(d_slot.at[s], d_sem.at[s])

        @pl.when(b >= 2)
        def _():
            wait_row_sent(b - 2)
            out_copy(b - 2).wait()

        tile = 2 * blk
        for m in range(seq // tile):
            sl = pl.ds(m * tile, tile)
            datt[sl, :] = lax.dot_general(d_slot[s, sl, :], wo[...], COL_CONTRACT, preferred_element_type=F32).astype(BF16)

        inv = inv_norms(b)
        for j in range(blocks):
            sl = pl.ds(j * blk, blk)
            for part in range(2):
                row = part * blocks + j
                scale = spread(inv[row:row + 1, :])
                col_inv[s, part, sl, :] = scale
                for h in range(heads):
                    cs = lane_cols(part, h)
                    rot[sl, cs] = turned(qk_ring[ring, sl, cs] * scale * gains[:, cs], sl, 0).astype(BF16)

        def head(h, carry):
            hq, hk, hv = (pl.ds(pl.multiple_of(n * cols + h * HEAD_DIM, HEAD_DIM), HEAD_DIM) for n in range(3))
            k_h, v_h = rot[:, hk], v_ring[s, :, hq]
            for j in range(blocks):
                sl = pl.ds(j * blk, blk)
                sc = lax.dot_general(rot[sl, hq], k_h, COL_CONTRACT, preferred_element_type=F32) * SCORE_SCALE
                p = jnp.exp2(sc - jnp.max(sc, axis=-1, keepdims=True))
                p = p * (1.0 / jnp.sum(p, axis=-1, keepdims=True))
                pb = p.astype(BF16)
                p_buf[sl, :] = pb
                o_stage[s, sl, hq] = jnp.dot(pb, v_h, preferred_element_type=F32).astype(BF16)
                dp = lax.dot_general(datt[sl, hq], v_h, COL_CONTRACT, preferred_element_type=F32)
                ds = (p * (dp - jnp.sum(p * dp, axis=-1, keepdims=True))).astype(BF16)
                ds_buf[sl, :] = ds
                dqk[sl, hq] = jnp.dot(ds, k_h, preferred_element_type=F32)
            dqk[:, hk] = lax.dot_general(ds_buf[...], rot[:, hq], ROW_CONTRACT, preferred_element_type=F32)
            dqkv_stage[s, :, hv] = lax.dot_general(p_buf[...], datt[:, hq], ROW_CONTRACT, preferred_element_type=F32).astype(BF16)
            return carry

        lax.fori_loop(0, heads, head, 0)

        for j in range(blocks):
            sl = pl.ds(j * blk, blk)
            for part in range(2):
                scale = col_inv[s, part, sl, :]
                total = None
                for h in range(heads):
                    cs = lane_cols(part, h)
                    dx = turned(dqk[sl, cs], sl, 3)
                    prod = dx * (qk_ring[ring, sl, cs] * scale)
                    dg_out[:, cs] = dg_out[:, cs] + jnp.sum(prod, axis=0, keepdims=True)
                    dqs[s, sl, cs] = dx * gains[:, cs]
                    prod = prod * gains[:, cs]
                    total = prod if total is None else total + prod
                stat_buf[me, b, pl.ds(part * blocks + j, 1), :] = jnp.sum(total.T, axis=0, keepdims=True)

        for n in range(3):
            cs = pl.ds(n * PANEL, PANEL)
            dwo_acc[:, cs] += lax.dot_general(o_stage[s], d_slot[s, :, cs], ROW_CONTRACT, preferred_element_type=F32)

    def finish(b):
        s, ring = even(b), lax.rem(b, 4)
        wait_bytes(stat_buf.at[pl.ds(0, PARTS - 1), b], stat_recv.at[b])
        inv = inv_norms(b)
        coef = jnp.sum(stat_buf[:, b], axis=0) * (1.0 / dim) * inv * inv
        for j in range(blocks):
            sl = pl.ds(j * blk, blk)
            for part in range(2):
                row = part * blocks + j
                scale = col_inv[s, part, sl, :]
                pull = spread(coef[row:row + 1, :])
                for h in range(heads):
                    cs = lane_cols(part, h)
                    dqkv_stage[s, sl, cs] = (scale * dqs[s, sl, cs] - pull * qk_ring[ring, sl, cs]).astype(BF16)
        out_copy(b).start()
        for n in range(3):
            cs = pl.ds(n * PANEL, PANEL)
            stage[:, cs] = lax.dot_general(dqkv_stage[s], w_all[cs, :], COL_CONTRACT, preferred_element_type=F32).astype(BF16)

    def pair_sum(b):
        wait_bytes(pair_in.at[b], pair_recv.at[b])
        load = pltpu.make_async_copy(pair_in.at[b], pair_buf, pair_load)
        load.start()

        @pl.when(b >= 1)
        def _():
            pair_copy(b - 1).wait()

        wait_bytes(pair_in.at[b], pair_send)
        load.wait()
        for n in range(4):
            pair_stage[even(b), n] = (stage[mine(peers.at[2 * n], seg), :].astype(F32) + pair_buf[n].astype(F32)).astype(BF16)
        pair_copy(b).start()

    def spread_wo(h):
        gw.complete(h)
        for t in peers.at[1:]:
            piece = gw.piece(h, t)
            remote(piece, piece, z_send, z_recv, {'dp': 1 - depth}).start()

    def half_sends(b):
        for n, t in enumerate((peers.y, peers.x)):
            remote(pair_out.at[b, 3, mine(n, seg // 2), :], half_out.at[b, n], half_send.at[b], half_recv.at[n, b], {'tp': t}).start()

    def early_halves(lo, hi):
        def work(b):
            for n in range(lo, hi):
                half_sends(n)
        return work

    def step(i, carry):
        stage_of(i, 4, rows, send_row)
        stage_of(i, rows, 1, early_halves(0, 3))
        stage_of(i, rows + 1, 1, early_halves(6, 9))
        stage_of(i, rows + 2, 1, early_halves(9, 11))
        stage_of(i, rows + 3, 1, early_halves(11, EARLY))
        stage_of(i + 1, 1, rows - 1, lambda b: gd.own(b + 1))
        stage_of(i, 0, rows, gy.direct)
        stage_of(i, 1, rows, gy.diagonal)
        stage_of(i, 2, rows, load_d)
        stage_of(i, 2, 1, lambda b: gw.own(depth))
        stage_of(i, 4, 1, lambda b: gw.direct(depth))
        stage_of(i, 5, 1, lambda b: gw.diagonal(depth))
        stage_of(i, 6, 1, lambda b: spread_wo(depth))
        stage_of(i, 2, rows, qkv)
        stage_of(i, 6, rows, pair_sum)
        stage_of(i, 5, rows, finish)
        stage_of(i, 2, rows, lambda b: send_sums(b, norm_buf, norm_send, norm_recv))
        stage_of(i, 5, rows, pair_sends)
        stage_of(i, rows, 1, early_halves(3, 6))
        stage_of(i + 2, 2, rows - 2, lambda b: gy.own(b + 2))
        stage_of(i, 0, rows, gd.direct)
        stage_of(i, 1, rows, gd.diagonal)
        stage_of(i, 1, rows, load_y)
        stage_of(i, 3, rows, attend)
        return carry

    keep_wo(0).start()
    keep_wo(1).start()
    lax.fori_loop(0, rows + 6, step, 0)
    stage[pl.ds(0, cols), :] = dwo_acc[...].astype(BF16)
    dwo_copy = pltpu.make_async_copy(stage.at[pl.ds(0, cols), :], dwo_out, dwo_sem)
    dwo_copy.start()
    keep_y.wait()
    keep_wo(0).wait()
    keep_wo(1).wait()
    for b in (rows - 2, rows - 1):
        wait_row_sent(b)
        out_copy(b).wait()
    pair_copy(rows - 1).wait()

    def drain(b, carry):
        gy.drain(b)
        gd.drain(b)
        return carry

    lax.fori_loop(0, rows, drain, 0)
    gw.drain(depth)
    others = pl.ds(0, PARTS - 1)
    for buf, sem in ((norm_buf, norm_send), (stat_buf, stat_send)):
        wait_bytes(buf.at[others], sem)
    wait_bytes(o_tok.at[pl.ds(0, rows - rows // PARTS)], o_recv)
    sent = wo_full.at[0, pl.ds(0, dim - cols), :]
    wait_bytes(sent, z_send)
    wait_bytes(sent, z_recv)
    dwo_copy.wait()
    for b in range(EARLY):
        wait_bytes(half_out.at[b], half_send.at[b])
        for n in range(2):
            wait_bytes(half_out.at[b, n], half_recv.at[n, b])


def attend_grad(y_loc, dp_loc, w_q, w_k, w_v, bias, gains, tabs, w_o):
    rows, seg, dim = y_loc.shape
    cols = w_o.shape[0]
    seq = seg * PARTS
    hbm = pl.BlockSpec(memory_space=pl.ANY)
    vmem = pl.BlockSpec(memory_space=pltpu.VMEM)
    dma = pltpu.SemaphoreType.DMA
    two, each = dma((2,)), dma((rows,))
    gathered = jax.ShapeDtypeStruct((rows, seq, dim), BF16)
    paired = jax.ShapeDtypeStruct((rows, 4, seg, dim), BF16)
    wide, all_cols = 2 * cols, 3 * cols
    return pl.pallas_call(
        attend_kernel,
        out_shape=(gathered, gathered, jax.ShapeDtypeStruct((rows, seq, all_cols), BF16), jax.ShapeDtypeStruct((rows, seg, dim), BF16),
                   jax.ShapeDtypeStruct((2, dim, dim // 2), BF16), jax.ShapeDtypeStruct((cols, dim), BF16), paired, paired,
                   jax.ShapeDtypeStruct((EARLY, 2, seg // 2, dim), BF16),
                   jax.ShapeDtypeStruct((1, wide), F32)),
        in_specs=[hbm] * 5 + [vmem] * 4,
        out_specs=[hbm] * 9 + [vmem],
        scratch_shapes=[pltpu.VMEM((dim, all_cols), BF16), pltpu.VMEM((seq, dim), BF16), pltpu.VMEM((2, seq, dim), BF16),
                        pltpu.VMEM((4, seq, wide), F32), pltpu.VMEM((2, seq, cols), BF16), pltpu.VMEM((seq, wide), BF16),
                        pltpu.VMEM((2, seq, cols), BF16), pltpu.VMEM((seq, cols), BF16), pltpu.VMEM((seq, wide), F32),
                        pltpu.VMEM((2, seq, wide), F32), pltpu.VMEM((2, seq, all_cols), BF16), pltpu.VMEM((2, 2, seq, HEAD_DIM), F32),
                        pltpu.VMEM((seq, seq), BF16), pltpu.VMEM((seq, seq), BF16), pltpu.VMEM((cols, dim), F32), pltpu.VMEM((seq, dim), BF16),
                        pltpu.VMEM((2, 4, seg, dim), BF16), pltpu.VMEM((4, seg, dim), BF16),
                        pltpu.VMEM((PARTS, rows, 8, HEAD_DIM), F32), pltpu.VMEM((PARTS, rows, 8, HEAD_DIM), F32)]
        + [[each] * 6, [each] * 6, [two] * 6, dma((3,)), dma, two, dma, dma, each, dma, each,
           two, two, dma, two, dma, each, dma, two, two, dma, dma, dma, dma((EARLY,)), dma((2, EARLY))],
        compiler_params=pltpu.CompilerParams(collective_id=0, has_side_effects=True, vmem_limit_bytes=VMEM_ALL),
        name='gather_attend',
    )(y_loc, dp_loc, w_q, w_k, w_v, bias, gains, tabs, w_o)


def scatter_kernel(pairs, halves, dqkv, y_full, o_tok, wo_full, x_loc, d_out, scale_rows, gate_rows, b_o,
                   xo_out, dx_out, mod_out, dw_out, half_in, last_in,
                   dt_slot, y_slot, dq_turned, half_stage, half_buf, last_buf, dw_acc,
                   o_all, x_all, dy_all, w_slot, proj, xo_stage, dx_stage, sums, mod_part, mod_in,
                   dt_sem, y_sem, half_send, last_send, half_recv0, half_recv1, last_recv0, last_recv1, half_load, last_load, dw_sem,
                   all_sem, wch_sem, xo_sem, dx_sem, part_send, part_recv, mod_send, mod_recv):
    peers = Peers()
    me = peers.me
    rows, seq, dim = y_full.shape
    seg = seq // PARTS
    half = seg // 2
    cols = dim // PARTS
    width = w_slot.shape[2]
    chunks = dim // width
    group = mod_part.shape[2]
    every = [pltpu.make_async_copy(src, dst, all_sem.at[n]) for n, (src, dst) in enumerate(((o_tok, o_all), (x_loc, x_all), (d_out, dy_all)))]

    def mine(b, size):
        return pl.ds(pl.multiple_of(b * size, size), size)

    def dt_copy(b):
        return pltpu.make_async_copy(dqkv.at[b], dt_slot.at[even(b)], dt_sem.at[even(b)])

    def y_copy(b):
        return pltpu.make_async_copy(y_full.at[b], y_slot.at[even(b)], y_sem.at[even(b)])

    def dx_copy(b):
        return pltpu.make_async_copy(dx_stage.at[even(b)], dx_out.at[b], dx_sem.at[even(b)])

    def chunk_copy(n):
        per = chunks // 2
        return pltpu.make_async_copy(wo_full.at[n // per, :, mine(lax.rem(n, per), width)], w_slot.at[even(n)], wch_sem.at[even(n)])

    def xo_copy(n):
        return pltpu.make_async_copy(xo_stage.at[even(n)], xo_out.at[:, :, mine(n, width)], xo_sem.at[even(n)])

    def remote(src, dst, send, recv, t):
        pltpu.make_async_remote_copy(src_ref=src, dst_ref=dst, send_sem=send, recv_sem=recv,
                                     device_id={'tp': t}, device_id_type=MESH).start()

    def half_sends(b):
        remote(pairs.at[b, 3, pl.ds(0, half), :], half_in.at[b, 0], half_send.at[b], half_recv0.at[b], peers.y)
        remote(pairs.at[b, 3, pl.ds(half, half), :], half_in.at[b, 1], half_send.at[b], half_recv1.at[b], peers.x)

    ring = half_stage.shape[0]

    def last_sends(b):
        s = lax.rem(b, ring)
        remote(half_stage.at[s, 0], last_in.at[b, 0], last_send.at[b], last_recv0.at[b], peers.x)
        remote(half_stage.at[s, 1], last_in.at[b, 1], last_send.at[b], last_recv1.at[b], peers.y)

    def half_loads(b, source=None):
        s = even(b)
        return (pltpu.make_async_copy((half_in if source is None else source).at[b], half_buf.at[s], half_load.at[0, s]),
                pltpu.make_async_copy(pairs.at[b, pl.ds(1, 2)], half_stage.at[lax.rem(b, ring)], half_load.at[1, s]))

    def last_loads(b):
        return (pltpu.make_async_copy(last_in.at[b], last_buf.at[pl.ds(0, 2)], last_load.at[0]),
                pltpu.make_async_copy(pairs.at[b, 0], last_buf.at[2], last_load.at[1]))

    def fetch_half(b):
        @pl.when(b >= ring)
        def _():
            wait_bytes(last_in.at[b - ring], last_send.at[b - ring])

        @pl.when(b < EARLY)
        def _():
            for c in half_loads(b, halves):
                c.start()

        @pl.when(b >= EARLY)
        def _():
            wait_bytes(half_in.at[b, 0], half_recv0.at[b])
            wait_bytes(half_in.at[b, 1], half_recv1.at[b])
            for c in half_loads(b):
                c.start()

    def half_sum(b):
        s, r = even(b), lax.rem(b, ring)
        for c in half_loads(b):
            c.wait()
        for n in range(2):
            sl = pl.ds(n * half, half)
            half_stage[r, n, sl, :] = (half_stage[r, n, sl, :].astype(F32) + half_buf[s, n].astype(F32)).astype(BF16)

    def fetch_last(b):
        wait_bytes(last_in.at[b, 0], last_recv0.at[b])
        wait_bytes(last_in.at[b, 1], last_recv1.at[b])
        for c in last_loads(b):
            c.start()

    def last_sum(b):
        for c in last_loads(b):
            c.wait()

        @pl.when(b >= 2)
        def _():
            dx_copy(b - 2).wait()

        sums[...] = jnp.zeros_like(sums)
        scale = scale_rows[pl.ds(b, 1), :]
        few = 16

        def tokens(n, carry):
            sl = mine(n, few)
            dy = last_buf[2, sl, :].astype(F32) + last_buf[0, sl, :].astype(F32) + last_buf[1, sl, :].astype(F32)
            x = x_all[b, sl, :].astype(F32)
            x = x - jnp.mean(x, axis=-1, keepdims=True)
            inv_std = lax.rsqrt(jnp.mean(x * x, axis=-1, keepdims=True) + EPS_NORM)
            x = x * inv_std
            sums[0] += dy
            sums[1] += dy * x
            dn = dy * scale
            pull = x * jnp.mean(dn * x, axis=-1, keepdims=True) + jnp.mean(dn, axis=-1, keepdims=True)
            dx_stage[even(b), sl, :] = (dy_all[b, sl, :].astype(F32) + inv_std * (dn - pull)).astype(BF16)
            return carry

        lax.fori_loop(0, seg // few, tokens, 0)
        dx_copy(b).start()
        for n in range(2):
            mod_part[b // group, n, pl.ds(lax.rem(b, group), 1), :] = jnp.sum(sums[n], axis=0, keepdims=True)

    def project_out(n):
        cs = mine(n, width)

        @pl.when(n == 0)
        def _():
            for c in every:
                c.wait()

        @pl.when(n >= 2)
        def _():
            xo_copy(n - 2).wait()

        chunk_copy(n).wait()
        flat = o_all[...].reshape(rows * seg, dim)
        proj[...] = (jnp.dot(flat, w_slot[even(n)], preferred_element_type=F32) + b_o[:, cs]).reshape(proj.shape)

        def row(b, carry):
            out = proj[b]
            xo_stage[even(n), b] = (x_all[b, :, cs].astype(F32) + gate_rows[pl.ds(b, 1), cs] * out).astype(BF16)
            mod_part[b // group, 2, pl.ds(lax.rem(b, group), 1), cs] = jnp.sum(dy_all[b, :, cs].astype(F32) * out, axis=0, keepdims=True)
            return carry

        lax.fori_loop(0, rows, row, 0)
        xo_copy(n).start()

        @pl.when(n + 2 < chunks)
        def _():
            chunk_copy(n + 2).start()

    def fetch_row(b):
        y_copy(b).start()
        dt_copy(b).start()

    def weight_grad(b):
        s = even(b)
        y_copy(b).wait()
        dt_copy(b).wait()
        dq_turned[...] = dt_slot[s].T
        for n in range(6):
            cs = pl.ds(n * (PANEL // 2), PANEL // 2)
            dw_acc[:, cs] += jnp.dot(dq_turned[...], y_slot[s, :, cs], preferred_element_type=F32)

    def share_parts(g):
        for t in peers.at[1:]:
            remote(mod_part.at[g, :, :, mine(t, cols)], mod_in.at[g, me], part_send.at[g], part_recv.at[g], t)
        mod_in[g, me] = mod_part[g, :, :, mine(me, cols)]

    def merge_parts(g):
        wait_bytes(mod_in.at[g, pl.ds(0, PARTS - 1)], part_recv.at[g])
        mod_out[g, :, :, mine(me, cols)] = jnp.sum(mod_in[g], axis=0)

    def share_mods(g):
        here = mod_out.at[g, :, :, mine(me, cols)]
        for t in peers.at[1:]:
            remote(here, here, mod_send.at[g], mod_recv.at[g], t)

    fetch_row(0)
    chunk_copy(0).start()
    chunk_copy(1).start()
    entry_barrier(peers, range(1, PARTS))
    for c in every:
        c.start()
    dw_acc[...] = jnp.zeros_like(dw_acc)

    def step(i, carry):
        stage_of(i, 1, rows, last_sends)
        stage_of(i + 4, EARLY, rows - EARLY, lambda b: half_sends(b + EARLY))
        stage_of(i, 0, rows, fetch_half)
        stage_of(i, rows, 1, share_parts)
        stage_of(i, 3, rows, fetch_last)
        stage_of(i + 1, 1, rows - 1, lambda b: fetch_row(b + 1))
        stage_of(i, 0, rows, weight_grad)
        stage_of(i, 0, rows, half_sum)
        stage_of(i, 1, chunks, project_out)
        stage_of(i, rows + 1, 1, merge_parts)
        stage_of(i, rows + 2, 1, share_mods)
        stage_of(i, 3, rows, last_sum)
        return carry

    lax.fori_loop(0, rows + 3, step, 0)
    share_parts(1)
    tile = dw_out.shape[0] // 3
    copies = [pltpu.make_async_copy(y_slot.at[n % 2, pl.ds(0, tile), :], dw_out.at[pl.ds(n * tile, tile), :], dw_sem.at[n]) for n in range(3)]
    for n, c in enumerate(copies):
        if n == 2:
            copies[0].wait()
        y_slot[n % 2, pl.ds(0, tile), :] = dw_acc[pl.ds(n * tile, tile), :].astype(BF16)
        c.start()
    merge_parts(1)
    share_mods(1)
    for c in copies[1:]:
        c.wait()
    for b in range(rows - ring, rows):
        wait_bytes(last_in.at[b], last_send.at[b])
    for n in range(2):
        dx_copy(rows - 1 - n).wait()
        xo_copy(chunks - 1 - n).wait()
    for b in range(EARLY, rows):
        wait_bytes(half_in.at[b], half_send.at[b])
    for g in range(2):
        some = mod_in.at[g, pl.ds(0, PARTS - 1)]
        wait_bytes(some, part_send.at[g])
        wait_bytes(some, mod_send.at[g])
        wait_bytes(some, mod_recv.at[g])


def scatter_grads(pairs, halves, dqkv, y_rows, o_rows, wo_full, x_loc, d_out, scale_rows, gate_rows, b_o):
    rows, seq, dim = y_rows.shape
    all_cols = dqkv.shape[2]
    seg = seq // PARTS
    group = rows // 2
    width = 256
    hbm = pl.BlockSpec(memory_space=pl.ANY)
    vmem = pl.BlockSpec(memory_space=pltpu.VMEM)
    dma = pltpu.SemaphoreType.DMA
    two, each = dma((2,)), dma((rows,))
    local = jax.ShapeDtypeStruct((rows, seg, dim), BF16)
    shard = pltpu.VMEM((rows, seg, dim), BF16)
    return pl.pallas_call(
        scatter_kernel,
        out_shape=(local, local, jax.ShapeDtypeStruct((2, 3, group, dim), F32), jax.ShapeDtypeStruct((all_cols, dim), BF16),
                   jax.ShapeDtypeStruct((rows, 2, seg // 2, dim), BF16), jax.ShapeDtypeStruct((rows, 2, seg, dim), BF16)),
        in_specs=[hbm] * 8 + [vmem] * 3,
        out_specs=[hbm] * 2 + [vmem] + [hbm] * 3,
        scratch_shapes=[pltpu.VMEM((2, seq, all_cols), BF16), pltpu.VMEM((2, seq, dim), BF16), pltpu.VMEM((all_cols, seq), BF16),
                        pltpu.VMEM((4, 2, seg, dim), BF16), pltpu.VMEM((2, 2, seg // 2, dim), BF16),
                        pltpu.VMEM((3, seg, dim), BF16), pltpu.VMEM((all_cols, dim), F32),
                        shard, shard, shard, pltpu.VMEM((2, dim, width), BF16), pltpu.VMEM((rows, seg, width), F32),
                        pltpu.VMEM((2, rows, seg, width), BF16), pltpu.VMEM((2, seg, dim), BF16), pltpu.VMEM((2, 16, dim), F32),
                        pltpu.VMEM((2, 3, group, dim), F32), pltpu.VMEM((2, PARTS, 3, group, dim // PARTS), F32)]
        + [two, two] + [each] * 6 + [dma((2, 2)), two, dma((3,)), dma((3,))] + [two] * 7,
        compiler_params=pltpu.CompilerParams(collective_id=1, has_side_effects=True, vmem_limit_bytes=VMEM_ALL),
        name='grad_scatter',
    )(pairs, halves, dqkv, y_rows, o_rows, wo_full, x_loc, d_out, scale_rows, gate_rows, b_o)


def solution(mesh):
    def device_step(x_loc, e_loc, m_block, w_q, b_q, w_k, b_k, w_v, b_v, w_o, b_o, g_q, g_k, pos_part, dy_loc):
        model_dim = x_loc.shape[-1]
        cols = w_q.shape[1]

        mod_rows = m_block[None] + e_loc
        shift_row = mod_rows[:, 0][:, None]
        scale_one = 1.0 + mod_rows[:, 1][:, None]
        gate_row = mod_rows[:, 2][:, None]
        x_float = x_loc.astype(jnp.float32)
        centered = x_float - jnp.mean(x_float, axis=-1, keepdims=True)
        inv_std = lax.rsqrt(jnp.mean(centered * centered, axis=-1, keepdims=True) + EPS_NORM)
        x_norm = centered * inv_std
        y_loc = (x_norm * scale_one + shift_row).astype(jnp.bfloat16)
        dy_float = dy_loc.astype(jnp.float32)
        dp_loc = (dy_float * gate_row).astype(jnp.bfloat16)
        y_rows, _, dqkv, o_rows, wo_full, d_wo, _, pairs, halves, d_gains = attend_grad(
            y_loc, dp_loc, w_q, w_k, w_v, jnp.concatenate([b_q, b_k, b_v])[None], jnp.concatenate([g_q, g_k])[None], rope_tables(pos_part), w_o)
        d_gq, d_gk = d_gains[0, :cols], d_gains[0, cols:]
        x_out, d_x, d_mods, dw_turned = scatter_grads(pairs, halves, dqkv, y_rows, o_rows, wo_full, x_loc, dy_loc,
                                                      scale_one[:, 0], gate_row[:, 0], b_o[None])[:4]
        d_wq, d_wk, d_wv = (dw_turned[n * cols:(n + 1) * cols].T for n in range(3))
        d_mod = jnp.moveaxis(d_mods, 1, 2).reshape(e_loc.shape)
        return (x_out, d_x, d_mod, jnp.sum(d_mod, axis=0), d_wq, d_wk, d_wv, d_wo, d_gq, d_gk)

    in_specs = (P('dp', 'tp', None), P('dp', None, None), P(None, None), P(None, 'tp'), P('tp'), P(None, 'tp'), P('tp'),
                P(None, 'tp'), P('tp'), P('tp', None), P(None), P('tp'), P('tp'), P('dp', None), P('dp', 'tp', None))
    out_specs = (P('dp', 'tp', None), P('dp', 'tp', None), P('dp', None, None), P('dp', None), P('dp', 'tp'), P('dp', 'tp'),
                 P('dp', 'tp'), P(('dp', 'tp'), None), P(('dp', 'tp')), P(('dp', 'tp')))
    return jax.shard_map(device_step, mesh=mesh, in_specs=in_specs, out_specs=out_specs, check_vma=False)
```

time: 1810 us -> 854 us (0.47)
  Pallas kernels: 0 us -> 790 us
  waiting for transfers between devices: 769 us -> 0 us
  matrix products: 642 us -> 0 us
  other arithmetic: 182 us -> 24.9 us
  local copies, waits for them, and re-layouts: 190 us -> 37 us
    pallas_call x0 -> x2, Pallas kernels: none -> 790 us  [the longest x1 606 us: attend_grad(): pl.pallas_call(attend_kernel, out_shape=(gathered, gathered, jax.ShapeDty...]
    dot_general x17 -> x0, matrix products: 606 us -> none  [the longest x3 89.4 us: attend(): jnp.einsum('bhqk,bkhd->bqhd', attn_probs, v_heads, preferred_element_type...]
    reduce_scatter x2 -> x0, waiting for transfers between devices: 384 us -> none  [the longest x1 272 us: device_step(): lax.psum_scatter(part_sum, 'tp', scatter_dimension=1, tiled=True)]
    all_gather x2 -> x0, waiting for transfers between devices: 361 us -> none  [the longest x1 221 us: device_step(): lax.all_gather(y_loc, 'tp', axis=1, tiled=True).reshape(rows_all, model_dim)]
    unnamed x78 -> x19, local copies, waits for them, and re-layouts: 118 us -> 25.5 us
    reshape x3, local copies, waits for them, and re-layouts: 49.5 us -> 2.22 us  [the longest x1 1.92 us: device_step(): d_mod = jnp.moveaxis(d_mods, 1, 2).reshape(e_loc.shape)]
    reduce_sum x4 -> x0, other arithmetic: 46.4 us -> none  [the longest x1 17.1 us: device_step(): d_gate = jnp.sum(dy_float * proj_loc, axis=1)]
    another operation x7 -> x1, other arithmetic: 44.9 us -> 0.73 us  [rope_tables(): jnp.stack([cos_tab, up, down, cos_tab * scale, -up * scale, -down * scale])]
  transfers between devices with their start and end apart: 7 -> 0, of which waited for: 6 -> 0; matrix products, arithmetic and copies ran while one was open for 23% -> 0% of each run, Pallas kernels for 0% -> 0%
where the time goes in v2:
time: 854 us; the launch traced here: 853 us
  Pallas kernels  790 us (93%)
  local copies, waits for them, and re-layouts  37 us (4%)
  other arithmetic  24.9 us (3%)
    pallas_call x1, Pallas kernels, attend_grad(): pl.pallas_call(attend_kernel, out_shape=(gathered, gathered, jax.ShapeDty...  606 us
    pallas_call x1, Pallas kernels, scatter_grads(): pl.pallas_call(scatter_kernel, out_shape=(local, local, jax.ShapeDtypeStr...  184 us
    unnamed x19, local copies, waits for them, and re-layouts  25.5 us

profile of v2, /device:TPU:0, one launch (start us, length us, event | category | flops | bytes accessed | tf_op | source)
XLA Modules:
  0.0 853.0 jit_solution(16692294069370659413)
XLA Ops:
  0.7 0.9 pad_maximum_fusion.1
  2.1 1.1 pad_maximum_fusion
  3.8 0.7 convert_element_type.53
  4.5 3.7 convert_reduce_fusion
  8.2 1.8 fusion.2
  11.6 0.8 constant_dynamic-update-slice_fusion
  12.4 0.7 fusion.6
  13.1 0.7 select_dynamic-update-slice_fusion
  13.8 0.7 multiply_dynamic-update-slice_fusion.2
  14.6 0.7 multiply_dynamic-update-slice_fusion.1
  15.3 0.7 multiply_dynamic-update-slice_fusion.tabs
  16.0 11.1 %fusion.5 = (bf16[16,64,3072]{2,1,0:T(8,128)(2,1)}, bf16[16,64,3072]{2,1,0:T(8,128)(2,1)}) fusion(bf16[16,64,3072]{2,1,0:T(8,128)(2,1)} %x_loc.1, f32[16,3072]{1,0:T(8,128)S(1)} %get-tuple-element.70, f32[16,3072]{1,0:T(8,128)S(1)} %get-tuple-element.71.scale_rows, f32[16,64]{1,0:T(8,128)S(1)} %add_rsqrt_fusion, f32[16,64]{1,0:T(8,128)S(1)} %broadcast_multiply_fusion, ...), kind=kLoop, calls=%fused_computation.7 | loop fusion | flops 28311552 | bytes 25763840 | tf_op jit(solution)/shard_map/convert_element_type | solution.py:745
  27.1 606.1 %gather_attend.1 = (bf16[16,512,3072]{2,1,0:T(8,128)(2,1)}, bf16[16,512,3072]{2,1,0:T(8,128)(2,1)}, bf16[16,512,1152]{2,1,0:T(8,128)(2,1)}, bf16[16,64,3072]{2,1...) custom-call(bf16[16,64,3072]{2,1,0:T(8,128)(2,1)} %get-tuple-element, ...), custom_call_target="tpu_custom_call" | custom-call | tf_op jit(solution)/shard_map/gather_attend/pallas_call | solution.py:452
  633.3 184.2 %grad_scatter.1 = (bf16[16,64,3072]{2,1,0:T(8,128)(2,1)}, bf16[16,64,3072]{2,1,0:T(8,128)(2,1)}, f32[2,3,8,3072]{3,2,1,0:T(8,128)}, bf16[1152,3072]{1,0:T(8,128)...) custom-call(bf16[16,4,64,3072]{3,2,1,0:T(8,128)(2,1)} %get-tuple-element.22.pairs, ...), custom_call_target="tpu_custom_call" | custom-call | tf_op jit(solution)/shard_map/grad_scatter/pallas_call | solution.py:714
  817.5 1.3 slice_reduce_fusion
  818.8 1.8 bitcast_reduce_fusion
  820.5 1.9 copy_bitcast_fusion
  822.5 5.8 slice_bitcast_fusion
  828.3 4.3 copy.45
  832.5 4.3 copy.44
  836.8 2.4 copy.43
  839.2 6.1 copy.55
  845.3 6.2 copy.56
  851.6 1.4 copy.57
  (30 shorter events, 2.7 us)
Async XLA Ops:
  0.6 7.6 copy-start
  8.2 3.2 copy-start.4
  8.2 3.2 copy-start.5
  11.6 15.5 %copy-start.2 = (f32[16,3072]{1,0:T(8,128)}, f32[16,3072]{1,0:T(8,128)S(1)}, u32[]{:S(2)}) copy-start(f32[16,3072]{1,0:T(8,128)S(1)} %get-tuple-element.69.gate_rows) | copy-start | bytes 589828
  11.6 15.5 %copy-start.3 = (f32[16,3072]{1,0:T(8,128)}, f32[16,3072]{1,0:T(8,128)S(1)}, u32[]{:S(2)}) copy-start(f32[16,3072]{1,0:T(8,128)S(1)} %get-tuple-element.71.scale_rows) | copy-start | bytes 589828
  845.3 6.2 copy-start.1

commit v3 on v2

--- a/solution.py
+++ b/solution.py
@@ -17,7 +17,8 @@
 BF16 = jnp.bfloat16
 PARTS = 8
 PANEL = 1024
-EARLY = 12
+EARLY = 14
+FEW = 16
 VMEM_ALL = 67043328
 SCORE_SCALE = HEAD_DIM ** -0.5 * 1.4426950408889634
 
@@ -36,13 +37,19 @@
     return jnp.cos(angles), jnp.sin(angles)
 
 
-def rope_tables(positions):
-    cos_tab, sin_tab = (jnp.repeat(t, 2, axis=1) for t in rope_angles(positions))
-    even = (jnp.arange(HEAD_DIM) % 2 == 0)[None]
-    up = jnp.where(even, -sin_tab, 0.0)
-    down = jnp.where(even, 0.0, sin_tab)
-    scale = HEAD_DIM ** -0.5
-    return jnp.stack([cos_tab, up, down, cos_tab * scale, -up * scale, -down * scale])
+def fill_tables(tabs, cos_tab, sin_tab):
+    odd = lax.rem(lax.broadcasted_iota(jnp.int32, (1, HEAD_DIM), 1), 2).astype(F32)
+    cos, sin = cos_tab[...].T, sin_tab[...].T
+    up = sin * (odd - 1.0)
+    down = sin * odd
+    for n, (tab, scale) in enumerate(((cos, 1.0), (up, -1.0), (down, -1.0))):
+        tabs[n] = tab
+        tabs[n + 3] = tab * (scale * HEAD_DIM ** -0.5)
+
+
+def fill_mods(mods, e_rows, m_rows):
+    for n in range(3):
+        mods[n] = e_rows[n] + m_rows[n:n + 1, :] + float(n == 1)
 
 
 class Peers:
@@ -138,16 +145,22 @@
         work(i - lag)
 
 
-def attend_kernel(y_loc, dp_loc, wq, wk, wv, bias, gains, tabs, wo,
-                  y_full, dp_full, dqkv_out, o_tok, wo_full, dwo_out, pair_in, pair_out, half_out, dg_out,
+def ahead_of(i, lead, count, work):
+    stage_of(i + lead, lead, count - lead, lambda b: work(b + lead))
+
+
+def attend_kernel(x_loc, d_out, wq, wk, wv, bq, bk, bv, gq, gk, cos_tab, sin_tab, wo, e_rows, m_rows,
+                  y_own, d_own, y_full, dp_full, dqkv_out, o_tok, wo_full, dwo_out, pair_in, pair_out, half_out, dg_out,
                   w_all, y_slot, d_slot, qk_ring, v_ring, rot, o_stage, datt, dqk, dqs, dqkv_stage, col_inv, p_buf, ds_buf,
                   dwo_acc, stage, pair_stage, pair_buf, norm_buf, stat_buf,
                   y_sems, d_sems, wo_sems, w_sem, y_sem, d_sem, keep_sem, norm_send, norm_recv, stat_send, stat_recv,
-                  o_send, o_keep, o_recv, out_sem, pair_send, pair_recv, pair_load, pair_sem, wo_keep, z_send, z_recv, dwo_sem, half_send, half_recv):
+                  o_send, o_keep, o_recv, out_sem, pair_send, pair_recv, pair_load, pair_sem, wo_keep, z_send, z_recv, dwo_sem, half_send, half_recv,
+                  raw, own_stage, raw_sem, own_sem, bias, gains, tabs, mods):
     peers = Peers()
     me = peers.me
     depth = lax.axis_index('dp')
-    rows, seg, dim = y_loc.shape
+    sums = (norm_buf, norm_send, norm_recv), (stat_buf, stat_send, stat_recv)
+    rows, seg, dim = x_loc.shape
     seq = seg * PARTS
     cols = wq.shape[1]
     heads = cols // HEAD_DIM
@@ -156,19 +169,65 @@
     wide = 2 * cols
     hemi = dim // 2
     weights = [pltpu.make_async_copy(w, w_all.at[:, pl.ds(n * cols, cols)], w_sem.at[n]) for n, w in enumerate((wq, wk, wv))]
+
+    def raw_copy(kind, b):
+        return pltpu.make_async_copy((x_loc, d_out)[kind].at[b], raw.at[kind, even(b)], raw_sem.at[kind, even(b)])
+
+    def own_copy(kind, b):
+        return pltpu.make_async_copy(own_stage.at[kind, even(b)], (y_own, d_own)[kind].at[b], own_sem.at[kind, even(b)])
+
+    for b in range(2):
+        raw_copy(0, b).start()
+        raw_copy(1, b).start()
     for c in weights:
         c.start()
+    fill_mods(mods, e_rows, m_rows)
     barrier = pltpu.get_barrier_semaphore()
     for t in peers.at[1:]:
         pl.semaphore_signal(barrier, inc=1, device_id={'tp': t}, device_id_type=MESH)
     pl.semaphore_signal(barrier, inc=1, device_id={'dp': 1 - depth}, device_id_type=MESH)
     pl.semaphore_wait(barrier, PARTS)
-    gy = RowGather(peers, lambda b: y_loc.at[b], y_full, y_sems, seg)
-    gd = RowGather(peers, lambda b: dp_loc.at[b], dp_full, d_sems, seg)
+    gy = RowGather(peers, lambda b: y_own.at[b], y_full, y_sems, seg)
+    gd = RowGather(peers, lambda b: d_own.at[b], dp_full, d_sems, seg)
     gw = RowGather(peers, lambda b: wo.at[:, pl.ds(pl.multiple_of(b * hemi, HEAD_DIM), hemi)], wo_full, wo_sems, cols)
-    gy.own(0)
-    gd.own(0)
-    gy.own(1)
+
+    def prepare(kind):
+        def work(b):
+            raw_copy(kind, b).wait()
+            s = even(b)
+            shift, scale, gate = (mods[n, pl.ds(b, 1), :] for n in range(3))
+            for n in range(seg // FEW):
+                sl = pl.ds(n * FEW, FEW)
+                x = raw[kind, s, sl, :].astype(F32)
+                if kind == 0:
+                    x = x - jnp.mean(x, axis=-1, keepdims=True)
+                    x = x * lax.rsqrt(jnp.mean(x * x, axis=-1, keepdims=True) + EPS_NORM)
+                    x = x * scale + shift
+                else:
+                    x = x * gate
+                own_stage[kind, s, sl, :] = x.astype(BF16)
+            own_copy(kind, b).start()
+
+            @pl.when(b + 2 < rows)
+            def _():
+                raw_copy(kind, b + 2).start()
+        return work
+
+    def own_row(kind):
+        def work(b):
+            own_copy(kind, b).wait()
+            (gy, gd)[kind].own(b)
+        return work
+
+    for kind, b in ((0, 0), (1, 0), (0, 1)):
+        prepare(kind)(b)
+        own_row(kind)(b)
+    prepare(1)(1)
+    fill_tables(tabs, cos_tab, sin_tab)
+    for n, part in enumerate((bq, bk, bv)):
+        bias[0, pl.ds(n * cols, cols)] = part[...]
+    for n, part in enumerate((gq, gk)):
+        gains[0, pl.ds(n * cols, cols)] = part[...]
     dwo_acc[...] = jnp.zeros_like(dwo_acc)
     dg_out[...] = jnp.zeros_like(dg_out)
     for c in weights:
@@ -197,12 +256,19 @@
     def remote(src, dst, send, recv, device):
         return pltpu.make_async_remote_copy(src_ref=src, dst_ref=dst, send_sem=send, recv_sem=recv, device_id=device, device_id_type=MESH)
 
-    def send_sums(b, buf, send, recv):
-        for t in peers.at[1:]:
-            remote(buf.at[me, b], buf.at[me, b], send, recv.at[b], {'tp': t}).start()
+    def share(n):
+        buf, send, recv = sums[n]
+
+        def work(b):
+            for t in peers.at[1:]:
+                remote(buf.at[me, b], buf.at[me, b], send, recv.at[b], {'tp': t}).start()
+        return work
+
+    def sum_of(n, b):
+        return jnp.sum(sums[n][0][:, b], axis=0) * (1.0 / dim)
 
     def send_row(b):
-        send_sums(b, stat_buf, stat_send, stat_recv)
+        share(1)(b)
         for t in peers.at[1:]:
             remote(o_rows(b, t), o_tok.at[b, :, mine(me, cols)], o_send.at[even(b)], o_recv, {'tp': t}).start()
         keep_o(b).start()
@@ -258,7 +324,7 @@
                 norm_buf[me, b, pl.ds(part * blocks + j, 1), :] = jnp.sum(total.T, axis=0, keepdims=True)
 
     def inv_norms(b):
-        return lax.rsqrt(jnp.sum(norm_buf[:, b], axis=0) * (1.0 / dim) + EPS_NORM)
+        return lax.rsqrt(sum_of(0, b) + EPS_NORM)
 
     def attend(b):
         s, ring = even(b), lax.rem(b, 4)
@@ -330,7 +396,7 @@
         s, ring = even(b), lax.rem(b, 4)
         wait_bytes(stat_buf.at[pl.ds(0, PARTS - 1), b], stat_recv.at[b])
         inv = inv_norms(b)
-        coef = jnp.sum(stat_buf[:, b], axis=0) * (1.0 / dim) * inv * inv
+        coef = sum_of(1, b) * inv * inv
         for j in range(blocks):
             sl = pl.ds(j * blk, blk)
             for part in range(2):
@@ -381,8 +447,11 @@
         stage_of(i, rows, 1, early_halves(0, 3))
         stage_of(i, rows + 1, 1, early_halves(6, 9))
         stage_of(i, rows + 2, 1, early_halves(9, 11))
-        stage_of(i, rows + 3, 1, early_halves(11, EARLY))
-        stage_of(i + 1, 1, rows - 1, lambda b: gd.own(b + 1))
+        stage_of(i, rows + 3, 1, early_halves(11, 12))
+        stage_of(i, rows + 4, 1, early_halves(12, 13))
+        stage_of(i, rows + 5, 1, early_halves(13, EARLY))
+        ahead_of(i, 2, rows, prepare(0))
+        ahead_of(i, 1, rows, own_row(1))
         stage_of(i, 0, rows, gy.direct)
         stage_of(i, 1, rows, gy.diagonal)
         stage_of(i, 2, rows, load_d)
@@ -393,10 +462,11 @@
         stage_of(i, 2, rows, qkv)
         stage_of(i, 6, rows, pair_sum)
         stage_of(i, 5, rows, finish)
-        stage_of(i, 2, rows, lambda b: send_sums(b, norm_buf, norm_send, norm_recv))
+        stage_of(i, 2, rows, share(0))
         stage_of(i, 5, rows, pair_sends)
         stage_of(i, rows, 1, early_halves(3, 6))
-        stage_of(i + 2, 2, rows - 2, lambda b: gy.own(b + 2))
+        ahead_of(i, 2, rows, prepare(1))
+        ahead_of(i, 2, rows, own_row(0))
         stage_of(i, 0, rows, gd.direct)
         stage_of(i, 1, rows, gd.diagonal)
         stage_of(i, 1, rows, load_y)
@@ -424,9 +494,8 @@
 
     lax.fori_loop(0, rows, drain, 0)
     gw.drain(depth)
-    others = pl.ds(0, PARTS - 1)
-    for buf, sem in ((norm_buf, norm_send), (stat_buf, stat_send)):
-        wait_bytes(buf.at[others], sem)
+    for buf, send, _ in sums:
+        wait_bytes(buf.at[pl.ds(0, PARTS - 1)], send)
     wait_bytes(o_tok.at[pl.ds(0, rows - rows // PARTS)], o_recv)
     sent = wo_full.at[0, pl.ds(0, dim - cols), :]
     wait_bytes(sent, z_send)
@@ -438,8 +507,8 @@
             wait_bytes(half_out.at[b, n], half_recv.at[n, b])
 
 
-def attend_grad(y_loc, dp_loc, w_q, w_k, w_v, bias, gains, tabs, w_o):
-    rows, seg, dim = y_loc.shape
+def attend_grad(x_loc, d_out, w_q, w_k, w_v, small, w_o, mod_parts):
+    rows, seg, dim = x_loc.shape
     cols = w_o.shape[0]
     seq = seg * PARTS
     hbm = pl.BlockSpec(memory_space=pl.ANY)
@@ -448,35 +517,40 @@
     two, each = dma((2,)), dma((rows,))
     gathered = jax.ShapeDtypeStruct((rows, seq, dim), BF16)
     paired = jax.ShapeDtypeStruct((rows, 4, seg, dim), BF16)
+    local = jax.ShapeDtypeStruct((rows, seg, dim), BF16)
+    local_ring = pltpu.VMEM((2, 2, seg, dim), BF16)
     wide, all_cols = 2 * cols, 3 * cols
+    partials = pltpu.VMEM((PARTS, rows, 8, HEAD_DIM), F32)
     return pl.pallas_call(
         attend_kernel,
-        out_shape=(gathered, gathered, jax.ShapeDtypeStruct((rows, seq, all_cols), BF16), jax.ShapeDtypeStruct((rows, seg, dim), BF16),
+        out_shape=(local, local, gathered, gathered, jax.ShapeDtypeStruct((rows, seq, all_cols), BF16), jax.ShapeDtypeStruct((rows, seg, dim), BF16),
                    jax.ShapeDtypeStruct((2, dim, dim // 2), BF16), jax.ShapeDtypeStruct((cols, dim), BF16), paired, paired,
                    jax.ShapeDtypeStruct((EARLY, 2, seg // 2, dim), BF16),
                    jax.ShapeDtypeStruct((1, wide), F32)),
-        in_specs=[hbm] * 5 + [vmem] * 4,
-        out_specs=[hbm] * 9 + [vmem],
+        in_specs=[hbm] * 5 + [vmem] * 10,
+        out_specs=[hbm] * 11 + [vmem],
         scratch_shapes=[pltpu.VMEM((dim, all_cols), BF16), pltpu.VMEM((seq, dim), BF16), pltpu.VMEM((2, seq, dim), BF16),
                         pltpu.VMEM((4, seq, wide), F32), pltpu.VMEM((2, seq, cols), BF16), pltpu.VMEM((seq, wide), BF16),
                         pltpu.VMEM((2, seq, cols), BF16), pltpu.VMEM((seq, cols), BF16), pltpu.VMEM((seq, wide), F32),
                         pltpu.VMEM((2, seq, wide), F32), pltpu.VMEM((2, seq, all_cols), BF16), pltpu.VMEM((2, 2, seq, HEAD_DIM), F32),
                         pltpu.VMEM((seq, seq), BF16), pltpu.VMEM((seq, seq), BF16), pltpu.VMEM((cols, dim), F32), pltpu.VMEM((seq, dim), BF16),
                         pltpu.VMEM((2, 4, seg, dim), BF16), pltpu.VMEM((4, seg, dim), BF16),
-                        pltpu.VMEM((PARTS, rows, 8, HEAD_DIM), F32), pltpu.VMEM((PARTS, rows, 8, HEAD_DIM), F32)]
+                        partials, partials]
         + [[each] * 6, [each] * 6, [two] * 6, dma((3,)), dma, two, dma, dma, each, dma, each,
-           two, two, dma, two, dma, each, dma, two, two, dma, dma, dma, dma((EARLY,)), dma((2, EARLY))],
+           two, two, dma, two, dma, each, dma, two, two, dma, dma, dma, dma((EARLY,)), dma((2, EARLY)),
+           local_ring, local_ring, dma((2, 2)), dma((2, 2)),
+           pltpu.VMEM((1, all_cols), F32), pltpu.VMEM((1, wide), F32), pltpu.VMEM((6, seq, HEAD_DIM), F32), pltpu.VMEM((3, rows, dim), F32)],
         compiler_params=pltpu.CompilerParams(collective_id=0, has_side_effects=True, vmem_limit_bytes=VMEM_ALL),
         name='gather_attend',
-    )(y_loc, dp_loc, w_q, w_k, w_v, bias, gains, tabs, w_o)
-
-
-def scatter_kernel(pairs, halves, dqkv, y_full, o_tok, wo_full, x_loc, d_out, scale_rows, gate_rows, b_o,
-                   xo_out, dx_out, mod_out, dw_out, half_in, last_in,
-                   dt_slot, y_slot, dq_turned, half_stage, half_buf, last_buf, dw_acc,
+    )(x_loc, d_out, w_q, w_k, w_v, *small, w_o, *mod_parts)
+
+
+def scatter_kernel(pairs, halves, dqkv, y_full, o_tok, wo_full, x_loc, d_out, e_rows, m_rows, b_o,
+                   xo_out, dx_out, mod_out, dwq_out, dwk_out, dwv_out, half_in, last_in,
+                   dt_slot, y_slot, half_stage, half_buf, last_buf, dw_acc,
                    o_all, x_all, dy_all, w_slot, proj, xo_stage, dx_stage, sums, mod_part, mod_in,
                    dt_sem, y_sem, half_send, last_send, half_recv0, half_recv1, last_recv0, last_recv1, half_load, last_load, dw_sem,
-                   all_sem, wch_sem, xo_sem, dx_sem, part_send, part_recv, mod_send, mod_recv):
+                   all_sem, wch_sem, xo_sem, dx_sem, part_send, part_recv, mod_send, mod_recv, mods):
     peers = Peers()
     me = peers.me
     rows, seq, dim = y_full.shape
@@ -571,24 +645,25 @@
             dx_copy(b - 2).wait()
 
         sums[...] = jnp.zeros_like(sums)
-        scale = scale_rows[pl.ds(b, 1), :]
-        few = 16
+        few = FEW // 2
+        scale = mods[1, pl.ds(b, 1), :]
 
         def tokens(n, carry):
-            sl = mine(n, few)
+            sl = mine(n, FEW)
             dy = last_buf[2, sl, :].astype(F32) + last_buf[0, sl, :].astype(F32) + last_buf[1, sl, :].astype(F32)
             x = x_all[b, sl, :].astype(F32)
             x = x - jnp.mean(x, axis=-1, keepdims=True)
             inv_std = lax.rsqrt(jnp.mean(x * x, axis=-1, keepdims=True) + EPS_NORM)
             x = x * inv_std
-            sums[0] += dy
-            sums[1] += dy * x
+            sums[0] += dy[:few] + dy[few:]
+            prod = dy * x
+            sums[1] += prod[:few] + prod[few:]
             dn = dy * scale
             pull = x * jnp.mean(dn * x, axis=-1, keepdims=True) + jnp.mean(dn, axis=-1, keepdims=True)
             dx_stage[even(b), sl, :] = (dy_all[b, sl, :].astype(F32) + inv_std * (dn - pull)).astype(BF16)
             return carry
 
-        lax.fori_loop(0, seg // few, tokens, 0)
+        lax.fori_loop(0, seg // FEW, tokens, 0)
         dx_copy(b).start()
         for n in range(2):
             mod_part[b // group, n, pl.ds(lax.rem(b, group), 1), :] = jnp.sum(sums[n], axis=0, keepdims=True)
@@ -611,7 +686,7 @@
 
         def row(b, carry):
             out = proj[b]
-            xo_stage[even(n), b] = (x_all[b, :, cs].astype(F32) + gate_rows[pl.ds(b, 1), cs] * out).astype(BF16)
+            xo_stage[even(n), b] = (x_all[b, :, cs].astype(F32) + mods[2, pl.ds(b, 1), cs] * out).astype(BF16)
             mod_part[b // group, 2, pl.ds(lax.rem(b, group), 1), cs] = jnp.sum(dy_all[b, :, cs].astype(F32) * out, axis=0, keepdims=True)
             return carry
 
@@ -630,10 +705,9 @@
         s = even(b)
         y_copy(b).wait()
         dt_copy(b).wait()
-        dq_turned[...] = dt_slot[s].T
         for n in range(6):
-            cs = pl.ds(n * (PANEL // 2), PANEL // 2)
-            dw_acc[:, cs] += jnp.dot(dq_turned[...], y_slot[s, :, cs], preferred_element_type=F32)
+            sl = pl.ds(n * (PANEL // 2), PANEL // 2)
+            dw_acc[sl, :] += lax.dot_general(y_slot[s, :, sl], dt_slot[s], ROW_CONTRACT, preferred_element_type=F32)
 
     def share_parts(g):
         for t in peers.at[1:]:
@@ -655,35 +729,50 @@
     entry_barrier(peers, range(1, PARTS))
     for c in every:
         c.start()
+    for b in range(EARLY, rows):
+        half_sends(b)
+    for b in range(2):
+        fetch_half(b)
+    fill_mods(mods, e_rows, m_rows)
+    half_sum(0)
+    half_sum(1)
+    fetch_half(2)
+    last_sends(0)
     dw_acc[...] = jnp.zeros_like(dw_acc)
+    half_sum(2)
+    last_sends(1)
 
     def step(i, carry):
-        stage_of(i, 1, rows, last_sends)
-        stage_of(i + 4, EARLY, rows - EARLY, lambda b: half_sends(b + EARLY))
-        stage_of(i, 0, rows, fetch_half)
-        stage_of(i, rows, 1, share_parts)
-        stage_of(i, 3, rows, fetch_last)
-        stage_of(i + 1, 1, rows - 1, lambda b: fetch_row(b + 1))
+        ahead_of(i, 2, rows, last_sends)
+        ahead_of(i, 3, rows, fetch_half)
+        stage_of(i, rows - 1, 1, share_parts)
+        ahead_of(i, 1, rows, fetch_row)
         stage_of(i, 0, rows, weight_grad)
-        stage_of(i, 0, rows, half_sum)
+        stage_of(i, 2, rows, fetch_last)
+        ahead_of(i, 3, rows, half_sum)
         stage_of(i, 1, chunks, project_out)
-        stage_of(i, rows + 1, 1, merge_parts)
-        stage_of(i, rows + 2, 1, share_mods)
-        stage_of(i, 3, rows, last_sum)
+        stage_of(i, rows, 1, merge_parts)
+        stage_of(i, rows + 1, 1, share_mods)
+        stage_of(i, 2, rows, last_sum)
         return carry
 
-    lax.fori_loop(0, rows + 3, step, 0)
+    lax.fori_loop(0, rows + 2, step, 0)
     share_parts(1)
-    tile = dw_out.shape[0] // 3
-    copies = [pltpu.make_async_copy(y_slot.at[n % 2, pl.ds(0, tile), :], dw_out.at[pl.ds(n * tile, tile), :], dw_sem.at[n]) for n in range(3)]
-    for n, c in enumerate(copies):
-        if n == 2:
-            copies[0].wait()
-        y_slot[n % 2, pl.ds(0, tile), :] = dw_acc[pl.ds(n * tile, tile), :].astype(BF16)
-        c.start()
+    tile = dt_slot.shape[1]
+    turns = dim // tile
+    own_cols = dwq_out.shape[1]
+    copies = [[pltpu.make_async_copy(dt_slot.at[n % 2, :, pl.ds(k * own_cols, own_cols)], out.at[pl.ds(n * tile, tile), :], dw_sem.at[n, k])
+               for k, out in enumerate((dwq_out, dwk_out, dwv_out))] for n in range(turns)]
+    for n in range(turns):
+        if n >= 2:
+            for c in copies[n - 2]:
+                c.wait()
+        dt_slot[n % 2] = dw_acc[pl.ds(n * tile, tile), :].astype(BF16)
+        for c in copies[n]:
+            c.start()
     merge_parts(1)
     share_mods(1)
-    for c in copies[1:]:
+    for c in copies[turns - 2] + copies[turns - 1]:
         c.wait()
     for b in range(rows - ring, rows):
         wait_bytes(last_in.at[b], last_send.at[b])
@@ -699,7 +788,7 @@
         wait_bytes(some, mod_recv.at[g])
 
 
-def scatter_grads(pairs, halves, dqkv, y_rows, o_rows, wo_full, x_loc, d_out, scale_rows, gate_rows, b_o):
+def scatter_grads(pairs, halves, dqkv, y_rows, o_rows, wo_full, x_loc, d_out, mod_parts, b_o):
     rows, seq, dim = y_rows.shape
     all_cols = dqkv.shape[2]
     seg = seq // PARTS
@@ -711,48 +800,36 @@
     two, each = dma((2,)), dma((rows,))
     local = jax.ShapeDtypeStruct((rows, seg, dim), BF16)
     shard = pltpu.VMEM((rows, seg, dim), BF16)
+    grad = jax.ShapeDtypeStruct((dim, all_cols // 3), BF16)
     return pl.pallas_call(
         scatter_kernel,
-        out_shape=(local, local, jax.ShapeDtypeStruct((2, 3, group, dim), F32), jax.ShapeDtypeStruct((all_cols, dim), BF16),
+        out_shape=(local, local, jax.ShapeDtypeStruct((2, 3, group, dim), F32), grad, grad, grad,
                    jax.ShapeDtypeStruct((rows, 2, seg // 2, dim), BF16), jax.ShapeDtypeStruct((rows, 2, seg, dim), BF16)),
         in_specs=[hbm] * 8 + [vmem] * 3,
-        out_specs=[hbm] * 2 + [vmem] + [hbm] * 3,
-        scratch_shapes=[pltpu.VMEM((2, seq, all_cols), BF16), pltpu.VMEM((2, seq, dim), BF16), pltpu.VMEM((all_cols, seq), BF16),
-                        pltpu.VMEM((4, 2, seg, dim), BF16), pltpu.VMEM((2, 2, seg // 2, dim), BF16),
-                        pltpu.VMEM((3, seg, dim), BF16), pltpu.VMEM((all_cols, dim), F32),
+        out_specs=[hbm] * 2 + [vmem] + [hbm] * 5,
+        scratch_shapes=[pltpu.VMEM((2, seq, all_cols), BF16), pltpu.VMEM((2, seq, dim), BF16),
+                        pltpu.VMEM((8, 2, seg, dim), BF16), pltpu.VMEM((2, 2, seg // 2, dim), BF16),
+                        pltpu.VMEM((3, seg, dim), BF16), pltpu.VMEM((dim, all_cols), F32),
                         shard, shard, shard, pltpu.VMEM((2, dim, width), BF16), pltpu.VMEM((rows, seg, width), F32),
-                        pltpu.VMEM((2, rows, seg, width), BF16), pltpu.VMEM((2, seg, dim), BF16), pltpu.VMEM((2, 16, dim), F32),
+                        pltpu.VMEM((2, rows, seg, width), BF16), pltpu.VMEM((2, seg, dim), BF16), pltpu.VMEM((2, FEW // 2, dim), F32),
                         pltpu.VMEM((2, 3, group, dim), F32), pltpu.VMEM((2, PARTS, 3, group, dim // PARTS), F32)]
-        + [two, two] + [each] * 6 + [dma((2, 2)), two, dma((3,)), dma((3,))] + [two] * 7,
+        + [two, two] + [each] * 6 + [dma((2, 2)), two, dma((dim // seq, 3)), dma((3,))] + [two] * 7 + [pltpu.VMEM((3, rows, dim), F32)],
         compiler_params=pltpu.CompilerParams(collective_id=1, has_side_effects=True, vmem_limit_bytes=VMEM_ALL),
         name='grad_scatter',
-    )(pairs, halves, dqkv, y_rows, o_rows, wo_full, x_loc, d_out, scale_rows, gate_rows, b_o)
+    )(pairs, halves, dqkv, y_rows, o_rows, wo_full, x_loc, d_out, *mod_parts, b_o)
 
 
 def solution(mesh):
     def device_step(x_loc, e_loc, m_block, w_q, b_q, w_k, b_k, w_v, b_v, w_o, b_o, g_q, g_k, pos_part, dy_loc):
-        model_dim = x_loc.shape[-1]
         cols = w_q.shape[1]
 
-        mod_rows = m_block[None] + e_loc
-        shift_row = mod_rows[:, 0][:, None]
-        scale_one = 1.0 + mod_rows[:, 1][:, None]
-        gate_row = mod_rows[:, 2][:, None]
-        x_float = x_loc.astype(jnp.float32)
-        centered = x_float - jnp.mean(x_float, axis=-1, keepdims=True)
-        inv_std = lax.rsqrt(jnp.mean(centered * centered, axis=-1, keepdims=True) + EPS_NORM)
-        x_norm = centered * inv_std
-        y_loc = (x_norm * scale_one + shift_row).astype(jnp.bfloat16)
-        dy_float = dy_loc.astype(jnp.float32)
-        dp_loc = (dy_float * gate_row).astype(jnp.bfloat16)
-        y_rows, _, dqkv, o_rows, wo_full, d_wo, _, pairs, halves, d_gains = attend_grad(
-            y_loc, dp_loc, w_q, w_k, w_v, jnp.concatenate([b_q, b_k, b_v])[None], jnp.concatenate([g_q, g_k])[None], rope_tables(pos_part), w_o)
+        mod_parts = (jnp.moveaxis(e_loc, 1, 0), m_block)
+        small = [b_q, b_k, b_v, g_q, g_k] + [jnp.repeat(t.T, 2, axis=0) for t in rope_angles(pos_part)]
+        _, _, y_rows, _, dqkv, o_rows, wo_full, d_wo, _, pairs, halves, d_gains = attend_grad(x_loc, dy_loc, w_q, w_k, w_v, small, w_o, mod_parts)
         d_gq, d_gk = d_gains[0, :cols], d_gains[0, cols:]
-        x_out, d_x, d_mods, dw_turned = scatter_grads(pairs, halves, dqkv, y_rows, o_rows, wo_full, x_loc, dy_loc,
-                                                      scale_one[:, 0], gate_row[:, 0], b_o[None])[:4]
-        d_wq, d_wk, d_wv = (dw_turned[n * cols:(n + 1) * cols].T for n in range(3))
+        x_out, d_x, d_mods, d_wq, d_wk, d_wv = scatter_grads(pairs, halves, dqkv, y_rows, o_rows, wo_full, x_loc, dy_loc, mod_parts, b_o[None])[:6]
         d_mod = jnp.moveaxis(d_mods, 1, 2).reshape(e_loc.shape)
-        return (x_out, d_x, d_mod, jnp.sum(d_mod, axis=0), d_wq, d_wk, d_wv, d_wo, d_gq, d_gk)
+        return (x_out, d_x, d_mod, jnp.sum(d_mods, axis=(0, 2)), d_wq, d_wk, d_wv, d_wo, d_gq, d_gk)
 
     in_specs = (P('dp', 'tp', None), P('dp', None, None), P(None, None), P(None, 'tp'), P('tp'), P(None, 'tp'), P('tp'),
                 P(None, 'tp'), P('tp'), P('tp', None), P(None), P('tp'), P('tp'), P('dp', None), P('dp', 'tp', None))

time: 854 us -> 803 us (0.940)
  other arithmetic: 24.9 us -> 2.6 us
  local copies, waits for them, and re-layouts: 37 us -> 21.7 us
  Pallas kernels: 790 us -> 777 us
    pallas_call x1, Pallas kernels: 184 us -> 169 us  [scatter_grads(): pl.pallas_call(scatter_kernel, out_shape=(local, local, jax.ShapeDtypeStr...]
    convert_element_type x1 -> x0, other arithmetic: 11.1 us -> none  [device_step(): y_loc = (x_norm * scale_one + shift_row).astype(jnp.bfloat16)]
    unnamed x19 -> x18, local copies, waits for them, and re-layouts: 25.5 us -> 15.9 us
where the time goes in v3:
time: 803 us; the launch traced here: 802 us
  Pallas kernels  777 us (97%)
  local copies, waits for them, and re-layouts  21.7 us (3%)
    pallas_call x1, Pallas kernels, attend_grad(): pl.pallas_call(attend_kernel, out_shape=(local, local, gathered, gathered...  608 us
    pallas_call x1, Pallas kernels, scatter_grads(): pl.pallas_call(scatter_kernel, out_shape=(local, local, jax.ShapeDtypeStr...  169 us

profile of v3, /device:TPU:0, one launch (start us, length us, event | category | flops | bytes accessed | tf_op | source)
XLA Modules:
  0.0 802.0 jit_solution(6269804931296155504)
XLA Ops:
  0.7 0.7 convert_element_type.37
  1.4 0.1 multiply_reduce_fusion
  1.5 0.5 sine_bitcast_fusion
  2.0 0.1 broadcast_in_dim.40
  2.1 0.9 reshape.90.sin_tab
  2.9 0.1 broadcast_in_dim.39
  3.0 0.9 reshape.89.cos_tab
  3.9 607.9 %gather_attend.1 = (bf16[16,64,3072]{2,1,0:T(8,128)(2,1)}, bf16[16,64,3072]{2,1,0:T(8,128)(2,1)}, bf16[16,512,3072]{2,1,0:T(8,128)(2,1)}, bf16[16,512,3072]{2,1,...) custom-call(bf16[16,64,3072]{2,1,0:T(8,128)(2,1)} %x_loc.3, ...), custom_call_target="tpu_custom_call" | custom-call | tf_op jit(solution)/shard_map/gather_attend/pallas_call | solution.py:524
  611.8 169.2 %grad_scatter.1 = (bf16[16,64,3072]{2,1,0:T(8,128)(2,1)}, bf16[16,64,3072]{2,1,0:T(8,128)(2,1)}, f32[2,3,8,3072]{3,2,1,0:T(8,128)}, bf16[3072,384]{1,0:T(8,128)(...) custom-call(bf16[16,4,64,3072]{3,2,1,0:T(8,128)(2,1)} %get-tuple-ele, ...), custom_call_target="tpu_custom_call" | custom-call | tf_op jit(solution)/shard_map/grad_scatter/pallas_call | solution.py:804
  781.0 1.3 slice_reduce_fusion
  782.2 1.8 reduce_sum.19
  784.0 2.1 copy_bitcast_fusion
  786.1 6.2 copy.36
  792.3 0.0 slice-done.1
  792.3 0.0 copy-start.2
  792.3 3.2 copy.37
  795.5 0.1 copy-done.3
  795.7 1.4 copy.38
  797.1 0.7 copy-done.2
  797.8 1.4 copy.39
  799.2 0.0 copy-done.1
  799.2 1.4 copy.40
  800.6 0.0 copy-done
  800.6 1.4 copy.41
  (10 shorter events, 0.0 us)
Async XLA Ops:
  784.0 8.3 %slice-start = ((s8[6291456]{0:T(1024)(128)(4,1)}), s8[4194304]{0:T(1024)(128)(4,1)S(1)}, s32[]{:S(2)}) async-start(s8[6291456]{0:T(1024)(128)(4,1)} %bitcast.11), calls=%async_computation | async-start | bytes 8388608
  786.1 6.3 slice-start.1
  792.3 3.3 copy-start.3
  792.3 5.4 copy-start.2
  795.7 3.5 copy-start.1
  795.7 4.9 copy-start

commit v4 on v3

--- a/solution.py
+++ b/solution.py
@@ -355,20 +355,18 @@
         def head(h, carry):
             hq, hk, hv = (pl.ds(pl.multiple_of(n * cols + h * HEAD_DIM, HEAD_DIM), HEAD_DIM) for n in range(3))
             k_h, v_h = rot[:, hk], v_ring[s, :, hq]
-            for j in range(blocks):
-                sl = pl.ds(j * blk, blk)
-                sc = lax.dot_general(rot[sl, hq], k_h, COL_CONTRACT, preferred_element_type=F32) * SCORE_SCALE
-                p = jnp.exp2(sc - jnp.max(sc, axis=-1, keepdims=True))
-                p = p * (1.0 / jnp.sum(p, axis=-1, keepdims=True))
-                pb = p.astype(BF16)
-                p_buf[sl, :] = pb
-                o_stage[s, sl, hq] = jnp.dot(pb, v_h, preferred_element_type=F32).astype(BF16)
-                dp = lax.dot_general(datt[sl, hq], v_h, COL_CONTRACT, preferred_element_type=F32)
-                ds = (p * (dp - jnp.sum(p * dp, axis=-1, keepdims=True))).astype(BF16)
-                ds_buf[sl, :] = ds
-                dqk[sl, hq] = jnp.dot(ds, k_h, preferred_element_type=F32)
-            dqk[:, hk] = lax.dot_general(ds_buf[...], rot[:, hq], ROW_CONTRACT, preferred_element_type=F32)
-            dqkv_stage[s, :, hv] = lax.dot_general(p_buf[...], datt[:, hq], ROW_CONTRACT, preferred_element_type=F32).astype(BF16)
+            for m in range(seq // tile):
+                sl = pl.ds(m * tile, tile)
+                sc = lax.dot_general(k_h, rot[sl, hq], COL_CONTRACT, preferred_element_type=F32) * SCORE_SCALE
+                p = jnp.exp2(sc - jnp.max(sc, axis=0, keepdims=True))
+                p = p * (1.0 / jnp.sum(p, axis=0, keepdims=True))
+                dp = lax.dot_general(v_h, datt[sl, hq], COL_CONTRACT, preferred_element_type=F32)
+                ds_buf[:, sl] = (p * (dp - jnp.sum(p * dp, axis=0, keepdims=True))).astype(BF16)
+                p_buf[:, sl] = p.astype(BF16)
+            dqk[:, hk] = jnp.dot(ds_buf[...], rot[:, hq], preferred_element_type=F32)
+            dqkv_stage[s, :, hv] = jnp.dot(p_buf[...], datt[:, hq], preferred_element_type=F32).astype(BF16)
+            o_stage[s, :, hq] = lax.dot_general(v_h, p_buf[...], ROW_CONTRACT, preferred_element_type=F32).T.astype(BF16)
+            dqk[:, hq] = lax.dot_general(k_h, ds_buf[...], ROW_CONTRACT, preferred_element_type=F32).T
             return carry
 
         lax.fori_loop(0, heads, head, 0)

time: 803 us -> 791 us (0.985)
  Pallas kernels: 777 us -> 766 us
    pallas_call x1, Pallas kernels: 608 us -> 596 us  [attend_grad(): pl.pallas_call(attend_kernel, out_shape=(local, local, gathered, gathered...]
where the time goes in v4:
time: 791 us; the launch traced here: 790 us
  Pallas kernels  766 us (97%)
  local copies, waits for them, and re-layouts  21.7 us (3%)
    pallas_call x1, Pallas kernels, attend_grad(): pl.pallas_call(attend_kernel, out_shape=(local, local, gathered, gathered...  596 us
    pallas_call x1, Pallas kernels, scatter_grads(): pl.pallas_call(scatter_kernel, out_shape=(local, local, jax.ShapeDtypeStr...  169 us
    unnamed x18, local copies, waits for them, and re-layouts  15.9 us

profile of v4, /device:TPU:0, one launch (start us, length us, event | category | flops | bytes accessed | tf_op | source)
XLA Modules:
  0.0 790.5 jit_solution(2203296443756007906)
XLA Ops:
  0.7 0.7 convert_element_type.37
  1.4 0.1 multiply_reduce_fusion
  1.5 0.5 sine_bitcast_fusion
  2.0 0.1 broadcast_in_dim.40
  2.1 0.9 reshape.90.sin_tab
  2.9 0.1 broadcast_in_dim.39
  3.0 0.9 reshape.89.cos_tab
  3.9 596.4 %gather_attend.1 = (bf16[16,64,3072]{2,1,0:T(8,128)(2,1)}, bf16[16,64,3072]{2,1,0:T(8,128)(2,1)}, bf16[16,512,3072]{2,1,0:T(8,128)(2,1)}, bf16[16,512,3072]{2,1,...) custom-call(bf16[16,64,3072]{2,1,0:T(8,128)(2,1)} %x_loc.3, ...), custom_call_target="tpu_custom_call" | custom-call | tf_op jit(solution)/shard_map/gather_attend/pallas_call | solution.py:522
  600.3 169.2 %grad_scatter.1 = (bf16[16,64,3072]{2,1,0:T(8,128)(2,1)}, bf16[16,64,3072]{2,1,0:T(8,128)(2,1)}, f32[2,3,8,3072]{3,2,1,0:T(8,128)}, bf16[3072,384]{1,0:T(8,128)(...) custom-call(bf16[16,4,64,3072]{3,2,1,0:T(8,128)(2,1)} %get-tuple-ele, ...), custom_call_target="tpu_custom_call" | custom-call | tf_op jit(solution)/shard_map/grad_scatter/pallas_call | solution.py:802
  769.4 1.3 slice_reduce_fusion
  770.7 1.8 reduce_sum.19
  772.5 2.1 copy_bitcast_fusion
  774.6 6.2 copy.36
  780.8 0.0 slice-done
  780.8 0.0 slice-done.1
  780.8 0.0 copy-start.2
  780.8 3.2 copy.37
  784.0 0.1 copy-done.3
  784.2 1.4 copy.38
  785.6 0.7 copy-done.2
  786.3 1.4 copy.39
  787.7 0.0 copy-done.1
  787.7 1.4 copy.40
  789.1 1.4 copy.41
  (10 shorter events, 0.0 us)
Async XLA Ops:
  772.5 8.3 %slice-start = ((s8[6291456]{0:T(1024)(128)(4,1)}), s8[4194304]{0:T(1024)(128)(4,1)S(1)}, s32[]{:S(2)}) async-start(s8[6291456]{0:T(1024)(128)(4,1)} %bitcast.11), calls=%async_computation | async-start | bytes 8388608
  774.6 6.3 slice-start.1
  780.8 3.3 copy-start.3
  780.8 5.4 copy-start.2
  784.2 3.5 copy-start.1
  784.2 4.9 copy-start

commit v5 on v4

--- a/solution.py
+++ b/solution.py
@@ -89,6 +89,10 @@
 
 def even(b):
     return lax.rem(b, 2)
+
+
+def third(b):
+    return lax.rem(b, 3)
 
 
 class RowGather:
@@ -245,10 +249,10 @@
         return pltpu.make_async_copy(pair_stage.at[even(b)], pair_out.at[b], pair_sem.at[even(b)])
 
     def o_rows(b, t):
-        return o_stage.at[even(b), mine(t, seg), :]
+        return o_stage.at[third(b), mine(t, seg), :]
 
     def keep_o(b):
-        return pltpu.make_async_copy(o_rows(b, me), o_tok.at[b, :, mine(me, cols)], o_keep.at[even(b)])
+        return pltpu.make_async_copy(o_rows(b, me), o_tok.at[b, :, mine(me, cols)], o_keep.at[third(b)])
 
     def keep_wo(h):
         return pltpu.make_async_copy(gw.src(h), wo_full.at[h, mine(me, cols), :], wo_keep.at[h])
@@ -268,13 +272,12 @@
         return jnp.sum(sums[n][0][:, b], axis=0) * (1.0 / dim)
 
     def send_row(b):
-        share(1)(b)
         for t in peers.at[1:]:
-            remote(o_rows(b, t), o_tok.at[b, :, mine(me, cols)], o_send.at[even(b)], o_recv, {'tp': t}).start()
+            remote(o_rows(b, t), o_tok.at[b, :, mine(me, cols)], o_send.at[third(b)], o_recv, {'tp': t}).start()
         keep_o(b).start()
 
     def wait_row_sent(b):
-        wait_bytes(o_stage.at[even(b), pl.ds(0, seq - seg), :], o_send.at[even(b)])
+        wait_bytes(o_stage.at[third(b), pl.ds(0, seq - seg), :], o_send.at[third(b)])
         keep_o(b).wait()
 
     def pair_sends(b):
@@ -331,9 +334,12 @@
         wait_bytes(norm_buf.at[pl.ds(0, PARTS - 1), b], norm_recv.at[b])
         wait_local(d_slot.at[s], d_sem.at[s])
 
+        @pl.when(b >= 3)
+        def _():
+            wait_row_sent(b - 3)
+
         @pl.when(b >= 2)
         def _():
-            wait_row_sent(b - 2)
             out_copy(b - 2).wait()
 
         tile = 2 * blk
@@ -365,7 +371,7 @@
                 p_buf[:, sl] = p.astype(BF16)
             dqk[:, hk] = jnp.dot(ds_buf[...], rot[:, hq], preferred_element_type=F32)
             dqkv_stage[s, :, hv] = jnp.dot(p_buf[...], datt[:, hq], preferred_element_type=F32).astype(BF16)
-            o_stage[s, :, hq] = lax.dot_general(v_h, p_buf[...], ROW_CONTRACT, preferred_element_type=F32).T.astype(BF16)
+            o_stage[third(b), :, hq] = lax.dot_general(v_h, p_buf[...], ROW_CONTRACT, preferred_element_type=F32).T.astype(BF16)
             dqk[:, hq] = lax.dot_general(k_h, ds_buf[...], ROW_CONTRACT, preferred_element_type=F32).T
             return carry
 
@@ -388,7 +394,7 @@
 
         for n in range(3):
             cs = pl.ds(n * PANEL, PANEL)
-            dwo_acc[:, cs] += lax.dot_general(o_stage[s], d_slot[s, :, cs], ROW_CONTRACT, preferred_element_type=F32)
+            dwo_acc[:, cs] += lax.dot_general(o_stage[third(b)], d_slot[s, :, cs], ROW_CONTRACT, preferred_element_type=F32)
 
     def finish(b):
         s, ring = even(b), lax.rem(b, 4)
@@ -441,34 +447,35 @@
         return work
 
     def step(i, carry):
-        stage_of(i, 4, rows, send_row)
         stage_of(i, rows, 1, early_halves(0, 3))
         stage_of(i, rows + 1, 1, early_halves(6, 9))
         stage_of(i, rows + 2, 1, early_halves(9, 11))
         stage_of(i, rows + 3, 1, early_halves(11, 12))
         stage_of(i, rows + 4, 1, early_halves(12, 13))
         stage_of(i, rows + 5, 1, early_halves(13, EARLY))
+        stage_of(i, 0, rows, gy.direct)
+        stage_of(i, 2, rows, gd.diagonal)
+        stage_of(i, 6, rows, pair_sum)
         ahead_of(i, 2, rows, prepare(0))
+        stage_of(i, 2, 1, lambda b: gw.own(depth))
+        stage_of(i, 4, rows, share(1))
         ahead_of(i, 1, rows, own_row(1))
-        stage_of(i, 0, rows, gy.direct)
-        stage_of(i, 1, rows, gy.diagonal)
-        stage_of(i, 2, rows, load_d)
-        stage_of(i, 2, 1, lambda b: gw.own(depth))
         stage_of(i, 4, 1, lambda b: gw.direct(depth))
+        stage_of(i, 2, rows, qkv)
         stage_of(i, 5, 1, lambda b: gw.diagonal(depth))
+        stage_of(i, 5, rows, send_row)
         stage_of(i, 6, 1, lambda b: spread_wo(depth))
-        stage_of(i, 2, rows, qkv)
-        stage_of(i, 6, rows, pair_sum)
         stage_of(i, 5, rows, finish)
-        stage_of(i, 2, rows, share(0))
-        stage_of(i, 5, rows, pair_sends)
         stage_of(i, rows, 1, early_halves(3, 6))
         ahead_of(i, 2, rows, prepare(1))
+        stage_of(i, 5, rows, pair_sends)
+        stage_of(i, 0, rows, gd.direct)
+        stage_of(i, 2, rows, load_d)
+        stage_of(i, 1, rows, load_y)
+        stage_of(i, 2, rows, share(0))
+        stage_of(i, 3, rows, attend)
+        stage_of(i, 0, rows, gy.diagonal)
         ahead_of(i, 2, rows, own_row(0))
-        stage_of(i, 0, rows, gd.direct)
-        stage_of(i, 1, rows, gd.diagonal)
-        stage_of(i, 1, rows, load_y)
-        stage_of(i, 3, rows, attend)
         return carry
 
     keep_wo(0).start()
@@ -480,6 +487,7 @@
     keep_y.wait()
     keep_wo(0).wait()
     keep_wo(1).wait()
+    wait_row_sent(rows - 3)
     for b in (rows - 2, rows - 1):
         wait_row_sent(b)
         out_copy(b).wait()
@@ -529,13 +537,13 @@
         out_specs=[hbm] * 11 + [vmem],
         scratch_shapes=[pltpu.VMEM((dim, all_cols), BF16), pltpu.VMEM((seq, dim), BF16), pltpu.VMEM((2, seq, dim), BF16),
                         pltpu.VMEM((4, seq, wide), F32), pltpu.VMEM((2, seq, cols), BF16), pltpu.VMEM((seq, wide), BF16),
-                        pltpu.VMEM((2, seq, cols), BF16), pltpu.VMEM((seq, cols), BF16), pltpu.VMEM((seq, wide), F32),
+                        pltpu.VMEM((3, seq, cols), BF16), pltpu.VMEM((seq, cols), BF16), pltpu.VMEM((seq, wide), F32),
                         pltpu.VMEM((2, seq, wide), F32), pltpu.VMEM((2, seq, all_cols), BF16), pltpu.VMEM((2, 2, seq, HEAD_DIM), F32),
                         pltpu.VMEM((seq, seq), BF16), pltpu.VMEM((seq, seq), BF16), pltpu.VMEM((cols, dim), F32), pltpu.VMEM((seq, dim), BF16),
                         pltpu.VMEM((2, 4, seg, dim), BF16), pltpu.VMEM((4, seg, dim), BF16),
                         partials, partials]
         + [[each] * 6, [each] * 6, [two] * 6, dma((3,)), dma, two, dma, dma, each, dma, each,
-           two, two, dma, two, dma, each, dma, two, two, dma, dma, dma, dma((EARLY,)), dma((2, EARLY)),
+           dma((3,)), dma((3,)), dma, two, dma, each, dma, two, two, dma, dma, dma, dma((EARLY,)), dma((2, EARLY)),
            local_ring, local_ring, dma((2, 2)), dma((2, 2)),
            pltpu.VMEM((1, all_cols), F32), pltpu.VMEM((1, wide), F32), pltpu.VMEM((6, seq, HEAD_DIM), F32), pltpu.VMEM((3, rows, dim), F32)],
         compiler_params=pltpu.CompilerParams(collective_id=0, has_side_effects=True, vmem_limit_bytes=VMEM_ALL),

time: 791 us -> 787 us (level)
  no operation moved by 1% of the time
where the time goes in v5:
time: 787 us
  Pallas kernels  762 us (97%)
  local copies, waits for them, and re-layouts  21.7 us (3%)
    pallas_call x1, Pallas kernels, attend_grad(): pl.pallas_call(attend_kernel, out_shape=(local, local, gathered, gathered...  592 us
    pallas_call x1, Pallas kernels, scatter_grads(): pl.pallas_call(scatter_kernel, out_shape=(local, local, jax.ShapeDtypeStr...  169 us
    unnamed x18, local copies, waits for them, and re-layouts  15.9 us

profile of v5, /device:TPU:0, one launch (start us, length us, event | category | flops | bytes accessed | tf_op | source)
XLA Modules:
  0.0 786.6 jit_solution(5768151105889977012)
XLA Ops:
  0.7 0.7 convert_element_type.37
  1.4 0.1 multiply_reduce_fusion
  1.5 0.5 sine_bitcast_fusion
  2.0 0.1 broadcast_in_dim.40
  2.1 0.9 reshape.90.sin_tab
  2.9 0.1 broadcast_in_dim.39
  3.0 0.9 reshape.89.cos_tab
  3.9 592.4 %gather_attend.1 = (bf16[16,64,3072]{2,1,0:T(8,128)(2,1)}, bf16[16,64,3072]{2,1,0:T(8,128)(2,1)}, bf16[16,512,3072]{2,1,0:T(8,128)(2,1)}, bf16[16,512,3072]{2,1,...) custom-call(bf16[16,64,3072]{2,1,0:T(8,128)(2,1)} %x_loc.3, ...), custom_call_target="tpu_custom_call" | custom-call | tf_op jit(solution)/shard_map/gather_attend/pallas_call | solution.py:530
  596.4 169.2 %grad_scatter.1 = (bf16[16,64,3072]{2,1,0:T(8,128)(2,1)}, bf16[16,64,3072]{2,1,0:T(8,128)(2,1)}, f32[2,3,8,3072]{3,2,1,0:T(8,128)}, bf16[3072,384]{1,0:T(8,128)(...) custom-call(bf16[16,4,64,3072]{3,2,1,0:T(8,128)(2,1)} %get-tuple-ele, ...), custom_call_target="tpu_custom_call" | custom-call | tf_op jit(solution)/shard_map/grad_scatter/pallas_call | solution.py:810
  765.5 1.3 slice_reduce_fusion
  766.8 1.8 reduce_sum.19
  768.6 2.1 copy_bitcast_fusion
  770.6 6.2 copy.36
  776.9 0.0 slice-done.1
  776.9 0.0 copy-start.2
  776.9 3.2 copy.37
  780.1 0.1 copy-done.3
  780.2 1.4 copy.38
  781.6 0.7 copy-done.2
  782.3 1.4 copy.39
  783.7 0.0 copy-done.1
  783.8 1.4 copy.40
  785.2 0.0 copy-done
  785.2 1.4 copy.41
  (10 shorter events, 0.0 us)
Async XLA Ops:
  768.6 8.3 %slice-start = ((s8[6291456]{0:T(1024)(128)(4,1)}), s8[4194304]{0:T(1024)(128)(4,1)S(1)}, s32[]{:S(2)}) async-start(s8[6291456]{0:T(1024)(128)(4,1)} %bitcast.11), calls=%async_computation | async-start | bytes 8388608
  770.6 6.3 slice-start.1
  776.9 3.3 copy-start.3
  776.9 5.4 copy-start.2
  780.2 3.5 copy-start.1
  780.2 4.9 copy-start
